TPU v7x, 128 devices: a whole 4x4x4 slice. The times are simulated.
128 devices in a mesh: attn: 4 (over z), expert: 32 (over y, x, core).
Axes of the slice: x: 4, y: 4, z: 4, core: 2. Of those that a mesh axis runs over, the one named last changes fastest.
Arguments:
- tokens: bfloat16 [1024, 4096], P(('attn', 'expert')), may hold values from -6 to 6
- expert_ids: int32 [1024, 8], P(('attn', 'expert')), may hold values from 0 to 63, all different within a row; in each aligned block of 8 rows (0 to 7, 8 to 15, ...) at most 3 rows name the same one
- route_gates: bfloat16 [1024, 8], P(('attn', 'expert')), may hold values from 0.049804688 to 0.59765625
- w_gate: bfloat16 [64, 4096, 1536], P('expert', None, 'attn'), may hold values from -0.09375 to 0.09375
- w_up: bfloat16 [64, 4096, 1536], P('expert', None, 'attn'), may hold values from -0.09375 to 0.09375
- w_down: bfloat16 [64, 1536, 4096], P('expert', 'attn'), may hold values from -0.15625 to 0.15625
Outputs:
- mixed: bfloat16 [1024, 4096], P(('attn', 'expert'))
Inputs may be any that keep to these rules, and one draw needn't show every extreme that they name: `expert_ids`: A token's 8 ids differ. Within one device's block of 8 tokens no expert is picked more than 3 times, and in every draw some expert is picked exactly 3 times in some block.
All inputs are finite; a program needn't handle non-finite values.
Results may differ from a plain program's by a relative error of at most 0.013.
Values may be sent and summed in bfloat16 or wider, within the bound.
No kernel may reach another device: no remote copies, remote signals or barrier semaphores. Data moves between devices by JAX's collectives and lax.ppermute only.
A program may use at most 128 MiB of HBM per device.

v0:
```python
import functools

import jax
import jax.numpy as jnp
from jax import lax
from jax.experimental import pallas as pl
from jax.experimental.pallas import tpu as pltpu
from jax.sharding import PartitionSpec as P


LONG = (0, 2)
AXES = ("attn", "expert")
NODES = [(z, y, x, core) for z in range(4) for y in range(4) for x in range(4) for core in range(2)]


def place(node):
    z, y, x, core = node
    return ((z * 4 + y) * 4 + x) * 2 + core


def pairs(step):
    moves = []
    for node in NODES:
        there = list(node)
        dim = LONG[node[3]]
        there[dim] = (there[dim] + step) % 4
        moves.append((place(node), place(there)))
    return moves


def planes():
    groups = {}
    for node in NODES:
        groups.setdefault((node[3], node[LONG[node[3]]]), []).append(place(node))
    return [groups[key] for key in sorted(groups)]


def move(value, step):
    return lax.ppermute(value, AXES, pairs(step))


def swap(value):
    return lax.ppermute(value, AXES, [(i, i ^ 1) for i in range(128)])


def in_plane(value):
    return lax.all_to_all(value, AXES, 0, 0, axis_index_groups=planes(), tiled=True)


def added(*terms):
    total = terms[0].astype(jnp.float32)
    for term in terms[1:]:
        total = total + term.astype(jnp.float32)
    return total.astype(jnp.bfloat16)


def expert_kernel(counts, local, width, hidden, loads, *refs):
    pieces = refs[: len(counts)]
    weights = refs[len(counts) : len(counts) + 3]
    own_ref, other_ref = refs[len(counts) + 3 : len(counts) + 5]
    scratch = refs[len(counts) + 5 :]
    copies = []
    if loads:
        held, (rows_ref, hidden_ref, sems) = scratch[:3], scratch[3:]
        for j in range(local):
            for kind in range(3):
                at = pl.ds(j * hidden, hidden) if kind == 2 else j
                copies.append(
                    pltpu.make_async_copy(
                        weights[kind].at[at], held[kind].at[at], sems.at[3 * j + kind]
                    )
                )
        for copy in (0, 1, 3, 4, 2, 5):
            copies[copy].start()
        weights = held
    else:
        rows_ref, hidden_ref = scratch
    gate_ref, up_ref, down_ref = weights
    start = 0
    for count, piece in zip(counts, pieces):
        rows_ref[start : start + count, :] = piece[...]
        start += count
    routing = rows_ref[:, width:].astype(jnp.float32)
    lane = lax.broadcasted_iota(jnp.int32, routing.shape, 1)
    first = (lax.axis_index("expert") * local).astype(jnp.float32)
    for j in range(local):
        hit = jnp.where((routing == first + j) & (lane < 8), 1.0, 0.0)
        weight = jnp.sum(pltpu.roll(hit, 8, 1) * routing, axis=1, keepdims=True)
        if loads:
            copies[3 * j].wait()
            copies[3 * j + 1].wait()
        inputs = rows_ref[:, :width]
        acts = []
        for part in range(3):
            if part == 0:
                columns = gate_ref[j, :, 0:256]
            elif part == 1:
                columns = jnp.concatenate([gate_ref[j, :, 256:384], up_ref[j, :, 0:128]], axis=1)
            else:
                columns = up_ref[j, :, 128:384]
            acts.append(jnp.dot(inputs, columns, preferred_element_type=jnp.float32))
        gates = [acts[0][:, :128], acts[0][:, 128:], acts[1][:, :128]]
        ups = [acts[1][:, 128:], acts[2][:, :128], acts[2][:, 128:]]
        for s in range(3):
            value = gates[s] / (1.0 + jnp.exp(-gates[s])) * ups[s] * weight
            at = j * hidden + s * 128
            hidden_ref[:, at : at + 128] = value.astype(jnp.bfloat16)
    if loads:
        for j in range(local):
            copies[3 * j + 2].wait()
    half = own_ref.shape[0]

    result = jnp.dot(hidden_ref[...], down_ref[...], preferred_element_type=jnp.float32)
    result = result.astype(jnp.bfloat16)
    own_ref[...] = result[:half]
    other_ref[...] = result[half:]


def experts(pieces, w_gate, w_up, w_down, loads=False):
    counts = tuple(piece.shape[0] for piece in pieces)
    total = sum(counts)
    local, width, hidden = w_gate.shape
    vmem = pl.BlockSpec(memory_space=pltpu.VMEM)
    space = pltpu.HBM if loads else pltpu.VMEM
    weights = [pltpu.with_memory_space_constraint(v, space) for v in (w_gate, w_up, w_down)]
    held = [pltpu.with_memory_space_constraint(v, pltpu.VMEM) for v in pieces]
    outs = [pltpu.VMEM((total // 2, width), jnp.bfloat16)] * 2
    scratch = [
        pltpu.VMEM((total, pieces[0].shape[1]), jnp.bfloat16),
        pltpu.VMEM((total, local * hidden), jnp.bfloat16),
    ]
    if loads:
        outs += [pltpu.VMEM(v.shape, v.dtype) for v in weights]
        scratch.append(pltpu.SemaphoreType.DMA((3 * local,)))
    return pl.pallas_call(
        functools.partial(expert_kernel, counts, local, width, hidden, loads),
        out_shape=outs,
        in_specs=[vmem] * len(counts) + [pl.BlockSpec(memory_space=pltpu.HBM) if loads else vmem] * 3,
        out_specs=[vmem] * len(outs),
        scratch_shapes=scratch,
        compiler_params=pltpu.CompilerParams(vmem_limit_bytes=16 << 20),
        cost_estimate=pl.CostEstimate(
            flops=6 * total * local * hidden * width,
            bytes_accessed=4 * total * width,
            transcendentals=total * local * hidden,
        ),
    )(*held, *weights)


def after(values, *others):
    return lax.optimization_barrier((*values, *others))[: len(values)]


def per_device(tokens, expert_ids, route_gates, w_gate, w_up, w_down):
    rows, width = tokens.shape
    picks = expert_ids.shape[1]
    local, _, hidden = w_gate.shape
    w_down = w_down.reshape(local * hidden, width)
    spare = jnp.zeros((rows, 128 - 2 * picks), tokens.dtype)
    block = jnp.concatenate([tokens, expert_ids.astype(tokens.dtype), route_gates, spare], axis=1)
    near = in_plane(jnp.broadcast_to(block[None], (16, *block.shape)))
    near = near.reshape(16 * rows, block.shape[1])
    half = 8 * rows
    near_a, near_b = near[:half], near[half:]
    ahead_a = move(near_a, -1)
    behind_b = move(near_b, 1)

    own0, other0, *weights = experts((near, swap(near)), w_gate, w_up, w_down, True)
    ahead_a, behind_b, near_a, near_b = after((ahead_a, behind_b, near_a, near_b), other0)
    far_a = move(ahead_a, -1)
    far_b = move(behind_b, 1)
    ahead_b = move(near_b, -1)
    behind_a = move(near_a, 1)
    pieces = (ahead_a, behind_b, swap(ahead_a), swap(behind_b))
    own1, other1 = experts(pieces, *weights)
    sum1 = added(own1, swap(other1))

    far_a, far_b = after((far_a, far_b), other1)
    pieces = (far_a, far_b, swap(far_a), swap(far_b))
    own2, other2 = experts(pieces, *weights)
    sum2 = added(own2, swap(other2))
    through_a = move(sum2[:half], -1)
    through_b = move(sum2[half:], 1)
    got_a = move(sum1[:half], 1)
    got_b = move(sum1[half:], -1)

    ahead_b, behind_a = after((ahead_b, behind_a), other2)
    pieces = (ahead_b, behind_a, swap(ahead_b), swap(behind_a))
    own3, other3 = experts(pieces, *weights)
    sum3 = added(own3, swap(other3))
    more_b = move(added(sum3[:half], through_b), 1)
    more_a = move(added(sum3[half:], through_a), -1)
    sum0 = added(own0, swap(other0))
    total = jnp.concatenate(
        [added(sum0[:half], got_a, more_a), added(sum0[half:], got_b, more_b)], axis=0
    )
    returned = in_plane(total.reshape(16, rows, width))
    return jnp.sum(returned.astype(jnp.float32), axis=0).astype(jnp.bfloat16)


def solution(mesh):
    placed = (
        P(AXES, None),
        P(AXES, None),
        P(AXES, None),
        P("expert", None, "attn"),
        P("expert", None, "attn"),
        P("expert", "attn", None),
    )

    return jax.shard_map(
        per_device, mesh=mesh, in_specs=placed, out_specs=P(AXES, None), check_vma=False
    )
```

profile of v0, /device:TPU:1, one launch (start us, length us, event | category | flops | bytes accessed | tf_op | source)
XLA Modules:
  0.0 118.4 jit_solution(13337414891092798762)
XLA Ops:
  0.0 0.7 convert_element_type.83
  0.7 0.9 concatenate.6
  1.7 26.3 %all_to_all.10 = bf16[16,8,4224]{2,1,0:T(8,128)(2,1)S(1)} all-to-all(bf16[16,8,4224]{2,1,0:T(8,128)(2,1)S(1)} %broadcast_in_dim.10), channel_id=1, replica_groups={{0,2,4,6,8,10,12,14,16,18,20,22,24,26,28,30},{32,34,36,38,40,42,44,46,4..., dimensions={0} | all-to-all | bytes 2162688 | tf_op jit(solution)/shard_map/all_to_all | solution.py:47
  28.1 2.5 %collective-permute-start.2 = (bf16[64,4224]{1,0:T(8,128)(2,1)S(1)}, bf16[64,4224]{1,0:T(8,128)(2,1)S(1)}, u32[]{:S(2)}, u32[]{:S(2)}) collective-permute-start(bf16[64,4224]{1,0:T(8,128)(2,1)S(1)} %get-tuple-element.34), channel_id=1, source_target_pairs={{0,96},{1,7},{2,98},{3,1},{4,100},{5,3},{6,102},{7,5},{8,104},{9,1... | collective-permute-start | bytes 1622024 | tf_op jit(solution)/shard_map/ppermute | solution.py:39
  30.7 9.4 %shard_map.64 = (bf16[128,4096]{1,0:T(8,128)(2,1)S(1)}, bf16[128,4096]{1,0:T(8,128)(2,1)S(1)}, bf16[2,4096,384]{2,1,0:T(8,128)(2,1)S(1)}, bf16[2,4096,384]{2,1,0:T(8,128)(2,1)S(1)}, bf16[768,4096]{1,0:T(8,128)(2,1)S(1)}) custom-call(bf16[128,4224]{1,0:T(8,128)(2,1)S(1)} %bitcast.9, bf16[128,4224]{1,0:T(8,128)(2,1)S(1)} %collective-permute-done.refs_1_, ...), custom_call_target="tpu_custom_call" | custom-call | flops 4831838208 | bytes 4194304 | tf_op jit(solution)/shard_map/pallas_call | solution.py:135
  40.3 0.3 collective-permute-start.5
  40.7 2.6 %collective-permute-start.10 = (bf16[64,4224]{1,0:T(8,128)(2,1)S(1)}, bf16[64,4224]{1,0:T(8,128)(2,1)S(1)}, u32[]{:S(2)}, u32[]{:S(2)}) collective-permute-start(bf16[64,4224]{1,0:T(8,128)(2,1)S(1)} %collective-permute-done.2.refs_0_), channel_id=1, source_target_pairs={{0,96},{1,7},{2,98},{3,1},{4,100},{5,3},{6,102},{7,5},{8,104},{9,1... | collective-permute-start | bytes 1622024 | tf_op jit(solution)/shard_map/ppermute | solution.py:39
  43.3 5.1 %shard_map.65 = (bf16[128,4096]{1,0:T(8,128)(2,1)S(1)}, bf16[128,4096]{1,0:T(8,128)(2,1)S(1)}) custom-call(bf16[64,4224]{1,0:T(8,128)(2,1)S(1)} %collective-permute-done.2.refs_0_, bf16[64,4224]{1,0:T(8,128)(2,1)S(1)} %collective-permute-done.3.refs_1_, bf16[64,4224]{1,0:T(8,128)(2,1)S(1)} %collective-permute-done.4.refs_2_, ...), custom_call_target="tpu_custom_call" | custom-call | flops 4831838208 | bytes 4194304 | tf_op jit(solution)/shard_map/pallas_call | solution.py:135
  48.5 1.1 collective-permute-done.10.refs_0_
  49.6 3.4 %collective-permute-done.11.refs_1_ = bf16[64,4224]{1,0:T(8,128)(2,1)S(1)} collective-permute-done((bf16[64,4224]{1,0:T(8,128)(2,1)S(1)}, bf16[64,4224]{1,0:T(8,128)(2,1)S(1)}, u32[]{:S(2)}, u32[]{:S(2)}) %collective-permute-start.11) | collective-permute-done | bytes 540704 | tf_op jit(solution)/shard_map/ppermute | solution.py:39
  53.0 0.6 collective-permute-start.12
  53.6 2.5 %collective-permute-start.8 = (bf16[64,4224]{1,0:T(8,128)(2,1)S(1)}, bf16[64,4224]{1,0:T(8,128)(2,1)S(1)}, u32[]{:S(2)}, u32[]{:S(2)}) collective-permute-start(bf16[64,4224]{1,0:T(8,128)(2,1)S(1)} %get-tuple-element.33), channel_id=1, source_target_pairs={{0,96},{1,7},{2,98},{3,1},{4,100},{5,3},{6,102},{7,5},{8,104},{9,1... | collective-permute-start | bytes 1622024 | tf_op jit(solution)/shard_map/ppermute | solution.py:39
  56.1 5.1 %shard_map.66 = (bf16[128,4096]{1,0:T(8,128)(2,1)S(1)}, bf16[128,4096]{1,0:T(8,128)(2,1)S(1)}) custom-call(bf16[64,4224]{1,0:T(8,128)(2,1)S(1)} %collective-permute-done.10.refs_0_, bf16[64,4224]{1,0:T(8,128)(2,1)S(1)} %collective-permute-done.11.refs_1_, bf16[64,4224]{1,0:T(8,128)(2,1)S(1)} %collective-permute-done.12.refs_2_, ...), custom_call_target="tpu_custom_call" | custom-call | flops 4831838208 | bytes 4194304 | tf_op jit(solution)/shard_map/pallas_call | solution.py:135
  61.2 0.5 collective-permute-start.17
  61.7 0.6 collective-permute-done.8.refs_0_
  62.3 3.1 %collective-permute-done.9.refs_1_ = bf16[64,4224]{1,0:T(8,128)(2,1)S(1)} collective-permute-done((bf16[64,4224]{1,0:T(8,128)(2,1)S(1)}, bf16[64,4224]{1,0:T(8,128)(2,1)S(1)}, u32[]{:S(2)}, u32[]{:S(2)}) %collective-permute-start.9) | collective-permute-done | bytes 540704 | tf_op jit(solution)/shard_map/ppermute | solution.py:39
  65.6 0.4 collective-permute-start.15
  66.3 1.2 %collective-permute-start.20 = (bf16[64,4096]{1,0:T(8,128)(2,1)S(1)}, bf16[64,4096]{1,0:T(8,128)(2,1)S(1)}, u32[]{:S(2)}, u32[]{:S(2)}) collective-permute-start(bf16[64,4096]{1,0:T(8,128)(2,1)S(1)} %get-tuple-element.48), channel_id=1, source_target_pairs={{0,96},{1,7},{2,98},{3,1},{4,100},{5,3},{6,102},{7,5},{8,104},{9,1... | collective-permute-start | bytes 1572872 | tf_op jit(solution)/shard_map/ppermute | solution.py:39
  67.8 0.3 collective-permute-done.15.refs_3_
  68.2 5.1 %shard_map.67 = (bf16[128,4096]{1,0:T(8,128)(2,1)S(1)}, bf16[128,4096]{1,0:T(8,128)(2,1)S(1)}) custom-call(bf16[64,4224]{1,0:T(8,128)(2,1)S(1)} %collective-permute-done.8.refs_0_, bf16[64,4224]{1,0:T(8,128)(2,1)S(1)} %collective-permute-done.9.refs_1_, bf16[64,4224]{1,0:T(8,128)(2,1)S(1)} %collective-permute-done.14.refs_2_, ...), custom_call_target="tpu_custom_call" | custom-call | flops 4831838208 | bytes 4194304 | tf_op jit(solution)/shard_map/pallas_call | solution.py:135
  73.3 0.4 collective-permute-start.16
  74.0 1.8 %collective-permute-start.18 = (bf16[64,4096]{1,0:T(8,128)(2,1)S(1)}, bf16[64,4096]{1,0:T(8,128)(2,1)S(1)}, u32[]{:S(2)}, u32[]{:S(2)}) collective-permute-start(bf16[64,4096]{1,0:T(8,128)(2,1)S(1)} %get-tuple-element.51), channel_id=1, source_target_pairs={{0,96},{1,7},{2,98},{3,1},{4,100},{5,3},{6,102},{7,5},{8,104},{9,1... | collective-permute-start | bytes 1572872 | tf_op jit(solution)/shard_map/ppermute | solution.py:39
  76.0 0.5 collective-permute-start.21
  76.7 5.7 %collective-permute-done.18 = bf16[64,4096]{1,0:T(8,128)(2,1)S(1)} collective-permute-done((bf16[64,4096]{1,0:T(8,128)(2,1)S(1)}, bf16[64,4096]{1,0:T(8,128)(2,1)S(1)}, u32[]{:S(2)}, u32[]{:S(2)}) %collective-permute-start.18) | collective-permute-done | bytes 524320 | tf_op jit(solution)/shard_map/ppermute | solution.py:39
  82.4 3.1 %collective-permute-done.21 = bf16[64,4096]{1,0:T(8,128)(2,1)S(1)} collective-permute-done((bf16[64,4096]{1,0:T(8,128)(2,1)S(1)}, bf16[64,4096]{1,0:T(8,128)(2,1)S(1)}, u32[]{:S(2)}, u32[]{:S(2)}) %collective-permute-start.21) | collective-permute-done | bytes 524320 | tf_op jit(solution)/shard_map/ppermute | solution.py:39
  85.8 0.9 collective-permute-start.19
  86.7 0.6 collective-permute-start.22
  87.6 6.6 %collective-permute-done.19 = bf16[64,4096]{1,0:T(8,128)(2,1)S(1)} collective-permute-done((bf16[64,4096]{1,0:T(8,128)(2,1)S(1)}, bf16[64,4096]{1,0:T(8,128)(2,1)S(1)}, u32[]{:S(2)}, u32[]{:S(2)}) %collective-permute-start.19) | collective-permute-done | bytes 524320 | tf_op jit(solution)/shard_map/ppermute | solution.py:39
  94.2 2.0 %collective-permute-done.22 = bf16[64,4096]{1,0:T(8,128)(2,1)S(1)} collective-permute-done((bf16[64,4096]{1,0:T(8,128)(2,1)S(1)}, bf16[64,4096]{1,0:T(8,128)(2,1)S(1)}, u32[]{:S(2)}, u32[]{:S(2)}) %collective-permute-start.22) | collective-permute-done | bytes 524320 | tf_op jit(solution)/shard_map/ppermute | solution.py:39
  96.2 0.5 add_convert_fusion.6
  96.8 20.8 %all_to_all.11 = bf16[16,8,4096]{2,1,0:T(8,128)(2,1)S(1)} all-to-all(bf16[16,8,4096]{2,1,0:T(8,128)(2,1)S(1)} %maximum_bitcast_fusion), channel_id=1, replica_groups={{0,2,4,6,8,10,12,14,16,18,20,22,24,26,28,30},{32,34,36,38,40,42,44,46,4..., dimensions={0} | all-to-all | bytes 2097152 | tf_op jit(solution)/shard_map/all_to_all | solution.py:47
  117.6 0.8 reduce_sum.12
  (35 shorter events, 2.7 us)
Async XLA Ops:
  28.0 2.7 %collective-permute-start = (bf16[128,4224]{1,0:T(8,128)(2,1)S(1)}, bf16[128,4224]{1,0:T(8,128)(2,1)S(1)}, u32[]{:S(2)}, u32[]{:S(2)}) collective-permute-start(bf16[128,4224]{1,0:T(8,128)(2,1)S(1)} %bitcast.8), channel_id=1, source_target_pairs={{0,1},{1,0},{2,3},{3,2},{4,5},{5,4},{6,7},{7,6},{8,9},{9,8},{10,11... | collective-permute-start | bytes 3244040 | tf_op jit(solution)/shard_map/ppermute | solution.py:43
  28.1 12.0 %collective-permute-start.2 = (bf16[64,4224]{1,0:T(8,128)(2,1)S(1)}, bf16[64,4224]{1,0:T(8,128)(2,1)S(1)}, u32[]{:S(2)}, u32[]{:S(2)}) collective-permute-start(bf16[64,4224]{1,0:T(8,128)(2,1)S(1)} %get-tuple-element.34), channel_id=1, source_target_pairs={{0,96},{1,7},{2,98},{3,1},{4,100},{5,3},{6,102},{7,5},{8,104},{9,1... | collective-permute-start | bytes 1622024 | tf_op jit(solution)/shard_map/ppermute | solution.py:39
  30.6 9.5 %collective-permute-start.3 = (bf16[64,4224]{1,0:T(8,128)(2,1)S(1)}, bf16[64,4224]{1,0:T(8,128)(2,1)S(1)}, u32[]{:S(2)}, u32[]{:S(2)}) collective-permute-start(bf16[64,4224]{1,0:T(8,128)(2,1)S(1)} %get-tuple-element.33), channel_id=1, source_target_pairs={{0,32},{1,3},{2,34},{3,5},{4,36},{5,7},{6,38},{7,1},{8,40},{9,11},... | collective-permute-start | bytes 1622024 | tf_op jit(solution)/shard_map/ppermute | solution.py:39
  40.1 3.2 %collective-permute-start.4 = (bf16[64,4224]{1,0:T(8,128)(2,1)S(1)}, bf16[64,4224]{1,0:T(8,128)(2,1)S(1)}, u32[]{:S(2)}, u32[]{:S(2)}) collective-permute-start(bf16[64,4224]{1,0:T(8,128)(2,1)S(1)} %collective-permute-done.2.refs_0_), channel_id=1, source_target_pairs={{0,1},{1,0},{2,3},{3,2},{4,5},{5,4},{6,7},{7,6},{8,9},{9,8},{10,11... | collective-permute-start | bytes 1622024 | tf_op jit(solution)/shard_map/ppermute | solution.py:43
  40.3 3.0 %collective-permute-start.5 = (bf16[64,4224]{1,0:T(8,128)(2,1)S(1)}, bf16[64,4224]{1,0:T(8,128)(2,1)S(1)}, u32[]{:S(2)}, u32[]{:S(2)}) collective-permute-start(bf16[64,4224]{1,0:T(8,128)(2,1)S(1)} %collective-permute-done.3.refs_1_), channel_id=1, source_target_pairs={{0,1},{1,0},{2,3},{3,2},{4,5},{5,4},{6,7},{7,6},{8,9},{9,8},{10,11... | collective-permute-start | bytes 1622024 | tf_op jit(solution)/shard_map/ppermute | solution.py:43
  40.7 8.9 %collective-permute-start.10 = (bf16[64,4224]{1,0:T(8,128)(2,1)S(1)}, bf16[64,4224]{1,0:T(8,128)(2,1)S(1)}, u32[]{:S(2)}, u32[]{:S(2)}) collective-permute-start(bf16[64,4224]{1,0:T(8,128)(2,1)S(1)} %collective-permute-done.2.refs_0_), channel_id=1, source_target_pairs={{0,96},{1,7},{2,98},{3,1},{4,100},{5,3},{6,102},{7,5},{8,104},{9,1... | collective-permute-start | bytes 1622024 | tf_op jit(solution)/shard_map/ppermute | solution.py:39
  43.3 9.7 %collective-permute-start.11 = (bf16[64,4224]{1,0:T(8,128)(2,1)S(1)}, bf16[64,4224]{1,0:T(8,128)(2,1)S(1)}, u32[]{:S(2)}, u32[]{:S(2)}) collective-permute-start(bf16[64,4224]{1,0:T(8,128)(2,1)S(1)} %collective-permute-done.3.refs_1_), channel_id=1, source_target_pairs={{0,32},{1,3},{2,34},{3,5},{4,36},{5,7},{6,38},{7,1},{8,40},{9,11},... | collective-permute-start | bytes 1622024 | tf_op jit(solution)/shard_map/ppermute | solution.py:39
  48.4 17.6 %collective-permute-start.6 = (bf16[128,4096]{1,0:T(8,128)(2,1)S(1)}, bf16[128,4096]{1,0:T(8,128)(2,1)S(1)}, u32[]{:S(2)}, u32[]{:S(2)}) collective-permute-start(bf16[128,4096]{1,0:T(8,128)(2,1)S(1)} %get-tuple-element.32), channel_id=1, source_target_pairs={{0,1},{1,0},{2,3},{3,2},{4,5},{5,4},{6,7},{7,6},{8,9},{9,8},{10,11... | collective-permute-start | bytes 3145736 | tf_op jit(solution)/shard_map/ppermute | solution.py:43
  53.0 3.1 %collective-permute-start.12 = (bf16[64,4224]{1,0:T(8,128)(2,1)S(1)}, bf16[64,4224]{1,0:T(8,128)(2,1)S(1)}, u32[]{:S(2)}, u32[]{:S(2)}) collective-permute-start(bf16[64,4224]{1,0:T(8,128)(2,1)S(1)} %collective-permute-done.10.refs_0_), channel_id=1, source_target_pairs={{0,1},{1,0},{2,3},{3,2},{4,5},{5,4},{6,7},{7,6},{8,9},{9,8},{10,11... | collective-permute-start | bytes 1622024 | tf_op jit(solution)/shard_map/ppermute | solution.py:43
  53.6 2.5 %collective-permute-start.13 = (bf16[64,4224]{1,0:T(8,128)(2,1)S(1)}, bf16[64,4224]{1,0:T(8,128)(2,1)S(1)}, u32[]{:S(2)}, u32[]{:S(2)}) collective-permute-start(bf16[64,4224]{1,0:T(8,128)(2,1)S(1)} %collective-permute-done.11.refs_1_), channel_id=1, source_target_pairs={{0,1},{1,0},{2,3},{3,2},{4,5},{5,4},{6,7},{7,6},{8,9},{9,8},{10,11... | collective-permute-start | bytes 1622024 | tf_op jit(solution)/shard_map/ppermute | solution.py:43
  53.6 8.8 %collective-permute-start.8 = (bf16[64,4224]{1,0:T(8,128)(2,1)S(1)}, bf16[64,4224]{1,0:T(8,128)(2,1)S(1)}, u32[]{:S(2)}, u32[]{:S(2)}) collective-permute-start(bf16[64,4224]{1,0:T(8,128)(2,1)S(1)} %get-tuple-element.33), channel_id=1, source_target_pairs={{0,96},{1,7},{2,98},{3,1},{4,100},{5,3},{6,102},{7,5},{8,104},{9,1... | collective-permute-start | bytes 1622024 | tf_op jit(solution)/shard_map/ppermute | solution.py:39
  56.0 9.4 %collective-permute-start.9 = (bf16[64,4224]{1,0:T(8,128)(2,1)S(1)}, bf16[64,4224]{1,0:T(8,128)(2,1)S(1)}, u32[]{:S(2)}, u32[]{:S(2)}) collective-permute-start(bf16[64,4224]{1,0:T(8,128)(2,1)S(1)} %get-tuple-element.34), channel_id=1, source_target_pairs={{0,32},{1,3},{2,34},{3,5},{4,36},{5,7},{6,38},{7,1},{8,40},{9,11},... | collective-permute-start | bytes 1622024 | tf_op jit(solution)/shard_map/ppermute | solution.py:39
  56.0 31.3 %collective-permute-start.1 = (bf16[128,4096]{1,0:T(8,128)(2,1)S(1)}, bf16[128,4096]{1,0:T(8,128)(2,1)S(1)}, u32[]{:S(2)}, u32[]{:S(2)}) collective-permute-start(bf16[128,4096]{1,0:T(8,128)(2,1)S(1)} %get-tuple-element.25), channel_id=1, source_target_pairs={{0,1},{1,0},{2,3},{3,2},{4,5},{5,4},{6,7},{7,6},{8,9},{9,8},{10,11... | collective-permute-start | bytes 3145736 | tf_op jit(solution)/shard_map/ppermute | solution.py:43
  61.2 12.5 %collective-permute-start.17 = (bf16[128,4096]{1,0:T(8,128)(2,1)S(1)}, bf16[128,4096]{1,0:T(8,128)(2,1)S(1)}, u32[]{:S(2)}, u32[]{:S(2)}) collective-permute-start(bf16[128,4096]{1,0:T(8,128)(2,1)S(1)} %get-tuple-element.37), channel_id=1, source_target_pairs={{0,1},{1,0},{2,3},{3,2},{4,5},{5,4},{6,7},{7,6},{8,9},{9,8},{10,11... | collective-permute-start | bytes 3145736 | tf_op jit(solution)/shard_map/ppermute | solution.py:43
  65.5 2.1 %collective-permute-start.14 = (bf16[64,4224]{1,0:T(8,128)(2,1)S(1)}, bf16[64,4224]{1,0:T(8,128)(2,1)S(1)}, u32[]{:S(2)}, u32[]{:S(2)}) collective-permute-start(bf16[64,4224]{1,0:T(8,128)(2,1)S(1)} %collective-permute-done.8.refs_0_), channel_id=1, source_target_pairs={{0,1},{1,0},{2,3},{3,2},{4,5},{5,4},{6,7},{7,6},{8,9},{9,8},{10,11... | collective-permute-start | bytes 1622024 | tf_op jit(solution)/shard_map/ppermute | solution.py:43
  65.6 2.6 %collective-permute-start.15 = (bf16[64,4224]{1,0:T(8,128)(2,1)S(1)}, bf16[64,4224]{1,0:T(8,128)(2,1)S(1)}, u32[]{:S(2)}, u32[]{:S(2)}) collective-permute-start(bf16[64,4224]{1,0:T(8,128)(2,1)S(1)} %collective-permute-done.9.refs_1_), channel_id=1, source_target_pairs={{0,1},{1,0},{2,3},{3,2},{4,5},{5,4},{6,7},{7,6},{8,9},{9,8},{10,11... | collective-permute-start | bytes 1622024 | tf_op jit(solution)/shard_map/ppermute | solution.py:43
  66.3 21.3 %collective-permute-start.20 = (bf16[64,4096]{1,0:T(8,128)(2,1)S(1)}, bf16[64,4096]{1,0:T(8,128)(2,1)S(1)}, u32[]{:S(2)}, u32[]{:S(2)}) collective-permute-start(bf16[64,4096]{1,0:T(8,128)(2,1)S(1)} %get-tuple-element.48), channel_id=1, source_target_pairs={{0,96},{1,7},{2,98},{3,1},{4,100},{5,3},{6,102},{7,5},{8,104},{9,1... | collective-permute-start | bytes 1572872 | tf_op jit(solution)/shard_map/ppermute | solution.py:39
  67.5 20.1 %collective-permute-start.7 = (bf16[64,4096]{1,0:T(8,128)(2,1)S(1)}, bf16[64,4096]{1,0:T(8,128)(2,1)S(1)}, u32[]{:S(2)}, u32[]{:S(2)}) collective-permute-start(bf16[64,4096]{1,0:T(8,128)(2,1)S(1)} %get-tuple-element.47), channel_id=1, source_target_pairs={{0,32},{1,3},{2,34},{3,5},{4,36},{5,7},{6,38},{7,1},{8,40},{9,11},... | collective-permute-start | bytes 1572872 | tf_op jit(solution)/shard_map/ppermute | solution.py:39
  73.3 2.7 %collective-permute-start.16 = (bf16[128,4096]{1,0:T(8,128)(2,1)S(1)}, bf16[128,4096]{1,0:T(8,128)(2,1)S(1)}, u32[]{:S(2)}, u32[]{:S(2)}) collective-permute-start(bf16[128,4096]{1,0:T(8,128)(2,1)S(1)} %get-tuple-element.41), channel_id=1, source_target_pairs={{0,1},{1,0},{2,3},{3,2},{4,5},{5,4},{6,7},{7,6},{8,9},{9,8},{10,11... | collective-permute-start | bytes 3145736 | tf_op jit(solution)/shard_map/ppermute | solution.py:43
  74.0 8.4 %collective-permute-start.18 = (bf16[64,4096]{1,0:T(8,128)(2,1)S(1)}, bf16[64,4096]{1,0:T(8,128)(2,1)S(1)}, u32[]{:S(2)}, u32[]{:S(2)}) collective-permute-start(bf16[64,4096]{1,0:T(8,128)(2,1)S(1)} %get-tuple-element.51), channel_id=1, source_target_pairs={{0,96},{1,7},{2,98},{3,1},{4,100},{5,3},{6,102},{7,5},{8,104},{9,1... | collective-permute-start | bytes 1572872 | tf_op jit(solution)/shard_map/ppermute | solution.py:39
  76.0 9.5 %collective-permute-start.21 = (bf16[64,4096]{1,0:T(8,128)(2,1)S(1)}, bf16[64,4096]{1,0:T(8,128)(2,1)S(1)}, u32[]{:S(2)}, u32[]{:S(2)}) collective-permute-start(bf16[64,4096]{1,0:T(8,128)(2,1)S(1)} %get-tuple-element.52), channel_id=1, source_target_pairs={{0,32},{1,3},{2,34},{3,5},{4,36},{5,7},{6,38},{7,1},{8,40},{9,11},... | collective-permute-start | bytes 1572872 | tf_op jit(solution)/shard_map/ppermute | solution.py:39
  85.8 8.4 %collective-permute-start.19 = (bf16[64,4096]{1,0:T(8,128)(2,1)S(1)}, bf16[64,4096]{1,0:T(8,128)(2,1)S(1)}, u32[]{:S(2)}, u32[]{:S(2)}) collective-permute-start(bf16[64,4096]{1,0:T(8,128)(2,1)S(1)} %get-tuple-element.49), channel_id=1, source_target_pairs={{0,96},{1,7},{2,98},{3,1},{4,100},{5,3},{6,102},{7,5},{8,104},{9,1... | collective-permute-start | bytes 1572872 | tf_op jit(solution)/shard_map/ppermute | solution.py:39
  86.7 9.5 %collective-permute-start.22 = (bf16[64,4096]{1,0:T(8,128)(2,1)S(1)}, bf16[64,4096]{1,0:T(8,128)(2,1)S(1)}, u32[]{:S(2)}, u32[]{:S(2)}) collective-permute-start(bf16[64,4096]{1,0:T(8,128)(2,1)S(1)} %get-tuple-element.50), channel_id=1, source_target_pairs={{0,32},{1,3},{2,34},{3,5},{4,36},{5,7},{6,38},{7,1},{8,40},{9,11},... | collective-permute-start | bytes 1572872 | tf_op jit(solution)/shard_map/ppermute | solution.py:39
where the time goes:
time: 119 us; the launch traced here: 118 us
  blocking collectives  47.1 us (40%)
  waiting for transfers between devices  26.3 us (22%)
  Pallas kernels  24.6 us (21%)
  starting transfers between devices  15.7 us (13%)
  other arithmetic  3.24 us (3%)
  local copies, waits for them, and re-layouts  1.23 us (1%)
    all_to_all x2, blocking collectives, in_plane(): lax.all_to_all(value, AXES, 0, 0, axis_index_groups=planes(), tiled=True)  47.1 us
    ppermute x12, waiting for transfers between devices, move(): return lax.ppermute(value, AXES, pairs(step))  25.7 us
    pallas_call x4, Pallas kernels, experts(): pl.pallas_call(functools.partial(expert_kernel, counts, local, width, hid...  24.6 us
    ppermute x12, starting transfers between devices, move(): return lax.ppermute(value, AXES, pairs(step))  13 us
    ppermute x11, starting transfers between devices, swap(): return lax.ppermute(value, AXES, [(i, i ^ 1) for i in range(128)])  2.76 us
  transfers between devices with their start and end apart: 23, of which 11 were waited for; matrix products, arithmetic and copies ran while one was open for 1% of the time, Pallas kernels for 21%

commit v1 on v0

v1 whole, which is shorter than its diff:
```python
import functools

import jax
import jax.numpy as jnp
from jax import lax
from jax.experimental import pallas as pl
from jax.experimental.pallas import tpu as pltpu
from jax.sharding import PartitionSpec as P


DIMS = ((2, 1, 0), (1, 0, 2))
AXES = ("attn", "expert")
NODES = [(z, y, x, core) for z in range(4) for y in range(4) for x in range(4) for core in range(2)]


def place(node):
    z, y, x, core = node
    return ((z * 4 + y) * 4 + x) * 2 + core


def pairs(phase, step):
    moves = []
    for node in NODES:
        there = list(node)
        dim = DIMS[node[3]][phase]
        there[dim] = (there[dim] + step) % 4
        moves.append((place(node), place(there)))
    return moves


def move(value, step, phase=2):
    return lax.ppermute(value, AXES, pairs(phase, step))


def swap(value):
    return lax.ppermute(value, AXES, [(i, i ^ 1) for i in range(128)])


def added(*terms):
    total = terms[0].astype(jnp.float32)
    for term in terms[1:]:
        total = total + term.astype(jnp.float32)
    return total.astype(jnp.bfloat16)


def load_kernel(count, *refs):
    sources, targets, sems = refs[:count], refs[count : 2 * count], refs[2 * count]
    copies = [pltpu.make_async_copy(sources[i], targets[i], sems.at[i]) for i in range(count)]
    for copy in copies:
        copy.start()
    for copy in copies:
        copy.wait()


def loaded(*weights):
    count = len(weights)
    return pl.pallas_call(
        functools.partial(load_kernel, count),
        out_shape=[pltpu.VMEM(v.shape, v.dtype) for v in weights],
        in_specs=[pl.BlockSpec(memory_space=pltpu.HBM)] * count,
        out_specs=[pl.BlockSpec(memory_space=pltpu.VMEM)] * count,
        scratch_shapes=[pltpu.SemaphoreType.DMA((count,))],
        compiler_params=pltpu.CompilerParams(vmem_limit_bytes=1 << 20),
        cost_estimate=pl.CostEstimate(flops=0, bytes_accessed=16_000_000, transcendentals=0),
    )(*[pltpu.with_memory_space_constraint(v, pltpu.HBM) for v in weights])


def expert_kernel(counts, local, width, hidden, *refs):
    pieces = refs[: len(counts)]
    gate_ref, up_ref, down_ref = refs[len(counts) : len(counts) + 3]
    own_ref, other_ref, rows_ref, hidden_ref = refs[len(counts) + 3 :]
    start = 0
    for count, piece in zip(counts, pieces):
        rows_ref[start : start + count, :] = piece[...]
        start += count
    routing = rows_ref[:, width:].astype(jnp.float32)
    lane = lax.broadcasted_iota(jnp.int32, routing.shape, 1)
    first = (lax.axis_index("expert") * local).astype(jnp.float32)
    for j in range(local):
        hit = jnp.where((routing == first + j) & (lane < 8), 1.0, 0.0)
        weight = jnp.sum(pltpu.roll(hit, 8, 1) * routing, axis=1, keepdims=True)
        inputs = rows_ref[:, :width]
        acts = []
        for part in range(3):
            if part == 0:
                columns = gate_ref[j, :, 0:256]
            elif part == 1:
                columns = jnp.concatenate([gate_ref[j, :, 256:384], up_ref[j, :, 0:128]], axis=1)
            else:
                columns = up_ref[j, :, 128:384]
            acts.append(jnp.dot(inputs, columns, preferred_element_type=jnp.float32))
        gates = [acts[0][:, :128], acts[0][:, 128:], acts[1][:, :128]]
        ups = [acts[1][:, 128:], acts[2][:, :128], acts[2][:, 128:]]
        for s in range(3):
            value = gates[s] / (1.0 + jnp.exp(-gates[s])) * ups[s] * weight
            at = j * hidden + s * 128
            hidden_ref[:, at : at + 128] = value.astype(jnp.bfloat16)
    half = own_ref.shape[0]

    result = jnp.dot(hidden_ref[...], down_ref[...], preferred_element_type=jnp.float32)
    result = result.astype(jnp.bfloat16)
    own_ref[...] = result[:half]
    other_ref[...] = result[half:]


def experts(pieces, w_gate, w_up, w_down):
    counts = tuple(piece.shape[0] for piece in pieces)
    total = sum(counts)
    local, width, hidden = w_gate.shape
    vmem = pl.BlockSpec(memory_space=pltpu.VMEM)
    held = [pltpu.with_memory_space_constraint(v, pltpu.VMEM) for v in (*pieces, w_gate, w_up, w_down)]
    return pl.pallas_call(
        functools.partial(expert_kernel, counts, local, width, hidden),
        out_shape=[pltpu.VMEM((total // 2, width), jnp.bfloat16)] * 2,
        in_specs=[vmem] * len(held),
        out_specs=[vmem] * 2,
        scratch_shapes=[
            pltpu.VMEM((total, pieces[0].shape[1]), jnp.bfloat16),
            pltpu.VMEM((total, local * hidden), jnp.bfloat16),
        ],
        compiler_params=pltpu.CompilerParams(vmem_limit_bytes=16 << 20),
        cost_estimate=pl.CostEstimate(
            flops=6 * total * local * hidden * width,
            bytes_accessed=4 * total * width,
            transcendentals=total * local * hidden,
        ),
    )(*held)


def after(values, *others):
    return lax.optimization_barrier((*values, *others))[: len(values)]


def per_device(tokens, expert_ids, route_gates, w_gate, w_up, w_down):
    rows, width = tokens.shape
    picks = expert_ids.shape[1]
    local, _, hidden = w_gate.shape
    half = 8 * rows
    spare = jnp.zeros((rows, 128 - 2 * picks), tokens.dtype)
    block = jnp.concatenate([tokens, expert_ids.astype(tokens.dtype), route_gates, spare], axis=1)
    (gate,) = loaded(w_gate)
    one = [move(block, -step, 0) for step in (1, 2, 3)]
    up, down = loaded(w_up, w_down.reshape(local * hidden, width))
    weights = (gate, up, down)
    block = jnp.concatenate([block] + one, axis=0)
    two = [move(block, -step, 1) for step in (1, 2, 3)]
    near_a = jnp.concatenate([block, two[0]], axis=0)
    near_b = jnp.concatenate([two[1], two[2]], axis=0)
    ahead_a = move(near_a, -1)
    behind_b = move(near_b, 1)

    own0, other0 = experts((near_a, near_b, swap(near_a), swap(near_b)), *weights)
    ahead_a, behind_b, near_a, near_b = after((ahead_a, behind_b, near_a, near_b), other0)
    far_a = move(ahead_a, -1)
    far_b = move(behind_b, 1)
    ahead_b = move(near_b, -1)
    behind_a = move(near_a, 1)
    pieces = (ahead_a, behind_b, swap(ahead_a), swap(behind_b))
    own1, other1 = experts(pieces, *weights)
    sum1 = added(own1, swap(other1))

    far_a, far_b = after((far_a, far_b), other1)
    pieces = (far_a, far_b, swap(far_a), swap(far_b))
    own2, other2 = experts(pieces, *weights)
    sum2 = added(own2, swap(other2))
    through_a = move(sum2[:half], -1)
    through_b = move(sum2[half:], 1)
    got_a = move(sum1[:half], 1)
    got_b = move(sum1[half:], -1)

    ahead_b, behind_a = after((ahead_b, behind_a), other2)
    pieces = (ahead_b, behind_a, swap(ahead_b), swap(behind_a))
    own3, other3 = experts(pieces, *weights)
    sum3 = added(own3, swap(other3))
    more_b = move(added(sum3[:half], through_b), 1)
    more_a = move(added(sum3[half:], through_a), -1)
    sum0 = added(own0, swap(other0))
    quarter = half // 2
    parts = []
    for side, got, more in ((sum0[:half], got_a, more_a), (sum0[half:], got_b, more_b)):
        for at in (0, quarter):
            parts.append(added(*[v[at : at + quarter] for v in (side, got, more)]))
    for phase in (1, 0):
        arrived = [move(parts[step], step, phase) for step in (1, 2, 3)]
        block = added(parts[0], *arrived)
        parts = [block[step * rows : (step + 1) * rows] for step in range(4)]
    return block


def solution(mesh):
    placed = (
        P(AXES, None),
        P(AXES, None),
        P(AXES, None),
        P("expert", None, "attn"),
        P("expert", None, "attn"),
        P("expert", "attn", None),
    )

    return jax.shard_map(
        per_device, mesh=mesh, in_specs=placed, out_specs=P(AXES, None), check_vma=False
    )
```

time: 119 us -> 117 us (0.983)
  the two profiles are of different devices: /device:TPU:1 before, /device:TPU:0 now
where the time goes in v1:
time: 117 us
  waiting for transfers between devices  48.9 us (42%)
  starting transfers between devices  35.8 us (31%)
  Pallas kernels  27.9 us (24%)
  other arithmetic  3.11 us (3%)
  local copies, waits for them, and re-layouts  1.22 us (1%)
    ppermute x24, waiting for transfers between devices, move(): return lax.ppermute(value, AXES, pairs(phase, step))  46.3 us
    ppermute x24, starting transfers between devices, move(): return lax.ppermute(value, AXES, pairs(phase, step))  33.2 us
    pallas_call x4, Pallas kernels, experts(): pl.pallas_call(functools.partial(expert_kernel, counts, local, width, hid...  20.4 us
    pallas_call x2, Pallas kernels, loaded(): pl.pallas_call(functools.partial(load_kernel, count), out_shape=[pltpu.VM...  7.42 us
    ppermute x12, starting transfers between devices, swap(): return lax.ppermute(value, AXES, [(i, i ^ 1) for i in range(128)])  2.65 us
    ppermute x12, waiting for transfers between devices, swap(): return lax.ppermute(value, AXES, [(i, i ^ 1) for i in range(128)])  2.58 us
    convert_element_type x8, other arithmetic, added(): return total.astype(jnp.bfloat16)  2.39 us
  transfers between devices with their start and end apart: 36, of which 21 were waited for; matrix products, arithmetic and copies ran while one was open for 1% of the time, Pallas kernels for 24%

profile of v1, /device:TPU:0, one launch (start us, length us, event | category | flops | bytes accessed | tf_op | source)
XLA Modules:
  0.0 117.2 jit_solution(8709743052557329317)
XLA Ops:
  1.6 2.9 %collective-permute-start = (bf16[8,4224]{1,0:T(8,128)(2,1)S(1)}, bf16[8,4224]{1,0:T(8,128)(2,1)S(1)}, u32[]{:S(2)}, u32[]{:S(2)}) collective-permute-start(bf16[8,4224]{1,0:T(8,128)(2,1)S(1)} %concatenate.13), channel_id=1, source_target_pairs={{0,6},{1,25},{2,0},{3,27},{4,2},{5,29},{6,4},{7,31},{8,14},{9,1},{... | collective-permute-start | bytes 202760 | tf_op jit(solution)/shard_map/ppermute | solution.py:32
  6.4 3.9 %collective-permute-done.1 = bf16[8,4224]{1,0:T(8,128)(2,1)S(1)} collective-permute-done((bf16[8,4224]{1,0:T(8,128)(2,1)S(1)}, bf16[8,4224]{1,0:T(8,128)(2,1)S(1)}, u32[]{:S(2)}, u32[]{:S(2)}) %collective-permute-start.1) | collective-permute-done | bytes 67616 | tf_op jit(solution)/shard_map/ppermute | solution.py:32
  11.0 3.3 %collective-permute-start.4 = (bf16[32,4224]{1,0:T(8,128)(2,1)S(1)}, bf16[32,4224]{1,0:T(8,128)(2,1)S(1)}, u32[]{:S(2)}, u32[]{:S(2)}) collective-permute-start(bf16[32,4224]{1,0:T(8,128)(2,1)S(1)} %pad_maximum_fusion), channel_id=1, source_target_pairs={{0,16},{1,65},{2,18},{3,67},{4,20},{5,69},{6,22},{7,71},{8,24},{9,... | collective-permute-start | bytes 811016 | tf_op jit(solution)/shard_map/ppermute | solution.py:32
  15.0 2.6 %collective-permute-start.3 = (bf16[32,4224]{1,0:T(8,128)(2,1)S(1)}, bf16[32,4224]{1,0:T(8,128)(2,1)S(1)}, u32[]{:S(2)}, u32[]{:S(2)}) collective-permute-start(bf16[32,4224]{1,0:T(8,128)(2,1)S(1)} %pad_maximum_fusion), channel_id=1, source_target_pairs={{0,24},{1,97},{2,26},{3,99},{4,28},{5,101},{6,30},{7,103},{8,0},{9... | collective-permute-start | bytes 811016 | tf_op jit(solution)/shard_map/ppermute | solution.py:32
  17.6 1.5 %collective-permute-done.4 = bf16[32,4224]{1,0:T(8,128)(2,1)S(1)} collective-permute-done((bf16[32,4224]{1,0:T(8,128)(2,1)S(1)}, bf16[32,4224]{1,0:T(8,128)(2,1)S(1)}, u32[]{:S(2)}, u32[]{:S(2)}) %collective-permute-start.4) | collective-permute-done | bytes 270368 | tf_op jit(solution)/shard_map/ppermute | solution.py:32
  19.1 2.9 %collective-permute-done.5 = bf16[32,4224]{1,0:T(8,128)(2,1)S(1)} collective-permute-done((bf16[32,4224]{1,0:T(8,128)(2,1)S(1)}, bf16[32,4224]{1,0:T(8,128)(2,1)S(1)}, u32[]{:S(2)}, u32[]{:S(2)}) %collective-permute-start.5) | collective-permute-done | bytes 270368 | tf_op jit(solution)/shard_map/ppermute | solution.py:32
  22.7 1.9 %collective-permute-start.10 = (bf16[64,4224]{1,0:T(8,128)(2,1)S(1)}, bf16[64,4224]{1,0:T(8,128)(2,1)S(1)}, u32[]{:S(2)}, u32[]{:S(2)}) collective-permute-start(bf16[64,4224]{1,0:T(8,128)(2,1)S(1)} %constant_dynamic-update-slice_fusion.5.refs_1_), channel_id=1, source_target_pairs={{0,32},{1,3},{2,34},{3,5},{4,36},{5,7},{6,38},{7,1},{8,40},{9,11},... | collective-permute-start | bytes 1622024 | tf_op jit(solution)/shard_map/ppermute | solution.py:32
  24.6 2.1 %collective-permute-start.9 = (bf16[64,4224]{1,0:T(8,128)(2,1)S(1)}, bf16[64,4224]{1,0:T(8,128)(2,1)S(1)}, u32[]{:S(2)}, u32[]{:S(2)}) collective-permute-start(bf16[64,4224]{1,0:T(8,128)(2,1)S(1)} %constant_dynamic-update-slice_fusion.refs_0_), channel_id=1, source_target_pairs={{0,96},{1,7},{2,98},{3,1},{4,100},{5,3},{6,102},{7,5},{8,104},{9,1... | collective-permute-start | bytes 1622024 | tf_op jit(solution)/shard_map/ppermute | solution.py:32
  26.7 2.8 %shard_map.64.refs_4_ = bf16[2,4096,384]{2,1,0:T(8,128)(2,1)S(1)} custom-call(bf16[2,4096,384]{2,1,0:T(8,128)(2,1)} %refs_0_.2), custom_call_target="tpu_custom_call" | custom-call | bytes 16000000 | tf_op jit(solution)/shard_map/pallas_call | solution.py:57
  29.5 4.6 %shard_map.65 = (bf16[2,4096,384]{2,1,0:T(8,128)(2,1)S(1)}, bf16[768,4096]{1,0:T(8,128)(2,1)S(1)}) custom-call(bf16[2,4096,384]{2,1,0:T(8,128)(2,1)} %refs_0_.3, bf16[768,4096]{1,0:T(8,128)(2,1)} %bitcast.1), custom_call_target="tpu_custom_call" | custom-call | bytes 16000000 | tf_op jit(solution)/shard_map/pallas_call | solution.py:57
  34.2 5.1 %shard_map.66 = (bf16[128,4096]{1,0:T(8,128)(2,1)S(1)}, bf16[128,4096]{1,0:T(8,128)(2,1)S(1)}) custom-call(bf16[64,4224]{1,0:T(8,128)(2,1)S(1)} %constant_dynamic-update-slice_fusion.refs_0_, bf16[64,4224]{1,0:T(8,128)(2,1)S(1)} %constant_dynamic-update-slice_fusion.5.refs_1_, bf16[64,4224]{1,0:T(8,128)(2,1)S(1)} %collective-permute-done.6.refs_2_, ...), custom_call_target="tpu_custom_call" | custom-call | flops 4831838208 | bytes 4194304 | tf_op jit(solution)/shard_map/pallas_call | solution.py:112
  39.9 2.5 %collective-permute-start.17 = (bf16[64,4224]{1,0:T(8,128)(2,1)S(1)}, bf16[64,4224]{1,0:T(8,128)(2,1)S(1)}, u32[]{:S(2)}, u32[]{:S(2)}) collective-permute-start(bf16[64,4224]{1,0:T(8,128)(2,1)S(1)} %collective-permute-done.9.refs_0_), channel_id=1, source_target_pairs={{0,96},{1,7},{2,98},{3,1},{4,100},{5,3},{6,102},{7,5},{8,104},{9,1... | collective-permute-start | bytes 1622024 | tf_op jit(solution)/shard_map/ppermute | solution.py:32
  42.4 5.1 %shard_map.67 = (bf16[128,4096]{1,0:T(8,128)(2,1)S(1)}, bf16[128,4096]{1,0:T(8,128)(2,1)S(1)}) custom-call(bf16[64,4224]{1,0:T(8,128)(2,1)S(1)} %collective-permute-done.9.refs_0_, bf16[64,4224]{1,0:T(8,128)(2,1)S(1)} %collective-permute-done.10.refs_1_, bf16[64,4224]{1,0:T(8,128)(2,1)S(1)} %collective-permute-done.11.refs_2_, ...), custom_call_target="tpu_custom_call" | custom-call | flops 4831838208 | bytes 4194304 | tf_op jit(solution)/shard_map/pallas_call | solution.py:112
  47.6 1.7 %collective-permute-done.17.refs_0_ = bf16[64,4224]{1,0:T(8,128)(2,1)S(1)} collective-permute-done((bf16[64,4224]{1,0:T(8,128)(2,1)S(1)}, bf16[64,4224]{1,0:T(8,128)(2,1)S(1)}, u32[]{:S(2)}, u32[]{:S(2)}) %collective-permute-start.17) | collective-permute-done | bytes 540704 | tf_op jit(solution)/shard_map/ppermute | solution.py:32
  49.3 3.7 %collective-permute-done.18.refs_1_ = bf16[64,4224]{1,0:T(8,128)(2,1)S(1)} collective-permute-done((bf16[64,4224]{1,0:T(8,128)(2,1)S(1)}, bf16[64,4224]{1,0:T(8,128)(2,1)S(1)}, u32[]{:S(2)}, u32[]{:S(2)}) %collective-permute-start.18) | collective-permute-done | bytes 540704 | tf_op jit(solution)/shard_map/ppermute | solution.py:32
  53.5 2.0 %collective-permute-start.16 = (bf16[64,4224]{1,0:T(8,128)(2,1)S(1)}, bf16[64,4224]{1,0:T(8,128)(2,1)S(1)}, u32[]{:S(2)}, u32[]{:S(2)}) collective-permute-start(bf16[64,4224]{1,0:T(8,128)(2,1)S(1)} %constant_dynamic-update-slice_fusion.refs_0_), channel_id=1, source_target_pairs={{0,32},{1,3},{2,34},{3,5},{4,36},{5,7},{6,38},{7,1},{8,40},{9,11},... | collective-permute-start | bytes 1622024 | tf_op jit(solution)/shard_map/ppermute | solution.py:32
  55.7 5.1 %shard_map.68 = (bf16[128,4096]{1,0:T(8,128)(2,1)S(1)}, bf16[128,4096]{1,0:T(8,128)(2,1)S(1)}) custom-call(bf16[64,4224]{1,0:T(8,128)(2,1)S(1)} %collective-permute-done.17.refs_0_, bf16[64,4224]{1,0:T(8,128)(2,1)S(1)} %collective-permute-done.18.refs_1_, bf16[64,4224]{1,0:T(8,128)(2,1)S(1)} %collective-permute-done.19.refs_2_, ...), custom_call_target="tpu_custom_call" | custom-call | flops 4831838208 | bytes 4194304 | tf_op jit(solution)/shard_map/pallas_call | solution.py:112
  61.2 1.6 %collective-permute-done.15.refs_0_ = bf16[64,4224]{1,0:T(8,128)(2,1)S(1)} collective-permute-done((bf16[64,4224]{1,0:T(8,128)(2,1)S(1)}, bf16[64,4224]{1,0:T(8,128)(2,1)S(1)}, u32[]{:S(2)}, u32[]{:S(2)}) %collective-permute-start.15) | collective-permute-done | bytes 540704 | tf_op jit(solution)/shard_map/ppermute | solution.py:32
  66.0 2.2 %collective-permute-start.28 = (bf16[64,4096]{1,0:T(8,128)(2,1)S(1)}, bf16[64,4096]{1,0:T(8,128)(2,1)S(1)}, u32[]{:S(2)}, u32[]{:S(2)}) collective-permute-start(bf16[64,4096]{1,0:T(8,128)(2,1)S(1)} %get-tuple-element.45), channel_id=1, source_target_pairs={{0,96},{1,7},{2,98},{3,1},{4,100},{5,3},{6,102},{7,5},{8,104},{9,1... | collective-permute-start | bytes 1572872 | tf_op jit(solution)/shard_map/ppermute | solution.py:32
  68.2 5.1 %shard_map.69 = (bf16[128,4096]{1,0:T(8,128)(2,1)S(1)}, bf16[128,4096]{1,0:T(8,128)(2,1)S(1)}) custom-call(bf16[64,4224]{1,0:T(8,128)(2,1)S(1)} %collective-permute-done.15.refs_0_, bf16[64,4224]{1,0:T(8,128)(2,1)S(1)} %collective-permute-done.16.refs_1_, bf16[64,4224]{1,0:T(8,128)(2,1)S(1)} %collective-permute-done.21.refs_2_, ...), custom_call_target="tpu_custom_call" | custom-call | flops 4831838208 | bytes 4194304 | tf_op jit(solution)/shard_map/pallas_call | solution.py:112
  73.9 2.2 %collective-permute-done.23 = bf16[128,4096]{1,0:T(8,128)(2,1)S(1)} collective-permute-done((bf16[128,4096]{1,0:T(8,128)(2,1)S(1)}, bf16[128,4096]{1,0:T(8,128)(2,1)S(1)}, u32[]{:S(2)}, u32[]{:S(2)}) %collective-permute-start.23) | collective-permute-done | bytes 1048608 | tf_op jit(solution)/shard_map/ppermute | solution.py:36
  76.4 6.7 %collective-permute-done.25 = bf16[64,4096]{1,0:T(8,128)(2,1)S(1)} collective-permute-done((bf16[64,4096]{1,0:T(8,128)(2,1)S(1)}, bf16[64,4096]{1,0:T(8,128)(2,1)S(1)}, u32[]{:S(2)}, u32[]{:S(2)}) %collective-permute-start.25) | collective-permute-done | bytes 524320 | tf_op jit(solution)/shard_map/ppermute | solution.py:32
  83.1 3.4 %collective-permute-done.29 = bf16[64,4096]{1,0:T(8,128)(2,1)S(1)} collective-permute-done((bf16[64,4096]{1,0:T(8,128)(2,1)S(1)}, bf16[64,4096]{1,0:T(8,128)(2,1)S(1)}, u32[]{:S(2)}, u32[]{:S(2)}) %collective-permute-start.29) | collective-permute-done | bytes 524320 | tf_op jit(solution)/shard_map/ppermute | solution.py:32
  86.9 2.0 %collective-permute-start.30 = (bf16[64,4096]{1,0:T(8,128)(2,1)S(1)}, bf16[64,4096]{1,0:T(8,128)(2,1)S(1)}, u32[]{:S(2)}, u32[]{:S(2)}) collective-permute-start(bf16[64,4096]{1,0:T(8,128)(2,1)S(1)} %get-tuple-element.47), channel_id=1, source_target_pairs={{0,32},{1,3},{2,34},{3,5},{4,36},{5,7},{6,38},{7,1},{8,40},{9,11},... | collective-permute-start | bytes 1572872 | tf_op jit(solution)/shard_map/ppermute | solution.py:32
  89.1 6.9 %collective-permute-done.26 = bf16[64,4096]{1,0:T(8,128)(2,1)S(1)} collective-permute-done((bf16[64,4096]{1,0:T(8,128)(2,1)S(1)}, bf16[64,4096]{1,0:T(8,128)(2,1)S(1)}, u32[]{:S(2)}, u32[]{:S(2)}) %collective-permute-start.26) | collective-permute-done | bytes 524320 | tf_op jit(solution)/shard_map/ppermute | solution.py:32
  97.6 1.6 %collective-permute-start.27 = (bf16[32,4096]{1,0:T(8,128)(2,1)S(1)}, bf16[32,4096]{1,0:T(8,128)(2,1)S(1)}, u32[]{:S(2)}, u32[]{:S(2)}) collective-permute-start(bf16[32,4096]{1,0:T(8,128)(2,1)S(1)} %get-tuple-element.43), channel_id=1, source_target_pairs={{0,8},{1,33},{2,10},{3,35},{4,12},{5,37},{6,14},{7,39},{8,16},{9,4... | collective-permute-start | bytes 786440 | tf_op jit(solution)/shard_map/ppermute | solution.py:32
  99.2 2.8 %collective-permute-start.31 = (bf16[32,4096]{1,0:T(8,128)(2,1)S(1)}, bf16[32,4096]{1,0:T(8,128)(2,1)S(1)}, u32[]{:S(2)}, u32[]{:S(2)}) collective-permute-start(bf16[32,4096]{1,0:T(8,128)(2,1)S(1)} %get-tuple-element.41), channel_id=1, source_target_pairs={{0,16},{1,65},{2,18},{3,67},{4,20},{5,69},{6,22},{7,71},{8,24},{9,... | collective-permute-start | bytes 786440 | tf_op jit(solution)/shard_map/ppermute | solution.py:32
  102.6 2.7 %collective-permute-done.27 = bf16[32,4096]{1,0:T(8,128)(2,1)S(1)} collective-permute-done((bf16[32,4096]{1,0:T(8,128)(2,1)S(1)}, bf16[32,4096]{1,0:T(8,128)(2,1)S(1)}, u32[]{:S(2)}, u32[]{:S(2)}) %collective-permute-start.27) | collective-permute-done | bytes 262176 | tf_op jit(solution)/shard_map/ppermute | solution.py:32
  105.3 3.9 %collective-permute-done.31 = bf16[32,4096]{1,0:T(8,128)(2,1)S(1)} collective-permute-done((bf16[32,4096]{1,0:T(8,128)(2,1)S(1)}, bf16[32,4096]{1,0:T(8,128)(2,1)S(1)}, u32[]{:S(2)}, u32[]{:S(2)}) %collective-permute-start.31) | collective-permute-done | bytes 262176 | tf_op jit(solution)/shard_map/ppermute | solution.py:32
  109.5 1.7 %collective-permute-start.34 = (bf16[8,4096]{1,0:T(8,128)(2,1)S(1)}, bf16[8,4096]{1,0:T(8,128)(2,1)S(1)}, u32[]{:S(2)}, u32[]{:S(2)}) collective-permute-start(bf16[8,4096]{1,0:T(8,128)(2,1)S(1)} %get-tuple-element.52), channel_id=1, source_target_pairs={{0,4},{1,17},{2,6},{3,19},{4,0},{5,21},{6,2},{7,23},{8,12},{9,25},... | collective-permute-start | bytes 196616 | tf_op jit(solution)/shard_map/ppermute | solution.py:32
  111.2 1.5 %collective-permute-start.35 = (bf16[8,4096]{1,0:T(8,128)(2,1)S(1)}, bf16[8,4096]{1,0:T(8,128)(2,1)S(1)}, u32[]{:S(2)}, u32[]{:S(2)}) collective-permute-start(bf16[8,4096]{1,0:T(8,128)(2,1)S(1)} %get-tuple-element.51), channel_id=1, source_target_pairs={{0,6},{1,25},{2,0},{3,27},{4,2},{5,29},{6,4},{7,31},{8,14},{9,1},{... | collective-permute-start | bytes 196616 | tf_op jit(solution)/shard_map/ppermute | solution.py:32
  112.8 2.9 %collective-permute-done.33 = bf16[8,4096]{1,0:T(8,128)(2,1)S(1)} collective-permute-done((bf16[8,4096]{1,0:T(8,128)(2,1)S(1)}, bf16[8,4096]{1,0:T(8,128)(2,1)S(1)}, u32[]{:S(2)}, u32[]{:S(2)}) %collective-permute-start.33) | collective-permute-done | bytes 65568 | tf_op jit(solution)/shard_map/ppermute | solution.py:32
  (68 shorter events, 15.9 us)
Async XLA Ops:
  1.6 4.8 %collective-permute-start = (bf16[8,4224]{1,0:T(8,128)(2,1)S(1)}, bf16[8,4224]{1,0:T(8,128)(2,1)S(1)}, u32[]{:S(2)}, u32[]{:S(2)}) collective-permute-start(bf16[8,4224]{1,0:T(8,128)(2,1)S(1)} %concatenate.13), channel_id=1, source_target_pairs={{0,6},{1,25},{2,0},{3,27},{4,2},{5,29},{6,4},{7,31},{8,14},{9,1},{... | collective-permute-start | bytes 202760 | tf_op jit(solution)/shard_map/ppermute | solution.py:32
  4.5 5.8 %collective-permute-start.1 = (bf16[8,4224]{1,0:T(8,128)(2,1)S(1)}, bf16[8,4224]{1,0:T(8,128)(2,1)S(1)}, u32[]{:S(2)}, u32[]{:S(2)}) collective-permute-start(bf16[8,4224]{1,0:T(8,128)(2,1)S(1)} %concatenate.13), channel_id=1, source_target_pairs={{0,4},{1,17},{2,6},{3,19},{4,0},{5,21},{6,2},{7,23},{8,12},{9,25},... | collective-permute-start | bytes 202760 | tf_op jit(solution)/shard_map/ppermute | solution.py:32
  5.3 5.7 %collective-permute-start.2 = (bf16[8,4224]{1,0:T(8,128)(2,1)S(1)}, bf16[8,4224]{1,0:T(8,128)(2,1)S(1)}, u32[]{:S(2)}, u32[]{:S(2)}) collective-permute-start(bf16[8,4224]{1,0:T(8,128)(2,1)S(1)} %concatenate.13), channel_id=1, source_target_pairs={{0,2},{1,9},{2,4},{3,11},{4,6},{5,13},{6,0},{7,15},{8,10},{9,17},{... | collective-permute-start | bytes 202760 | tf_op jit(solution)/shard_map/ppermute | solution.py:32
  11.0 8.0 %collective-permute-start.4 = (bf16[32,4224]{1,0:T(8,128)(2,1)S(1)}, bf16[32,4224]{1,0:T(8,128)(2,1)S(1)}, u32[]{:S(2)}, u32[]{:S(2)}) collective-permute-start(bf16[32,4224]{1,0:T(8,128)(2,1)S(1)} %pad_maximum_fusion), channel_id=1, source_target_pairs={{0,16},{1,65},{2,18},{3,67},{4,20},{5,69},{6,22},{7,71},{8,24},{9,... | collective-permute-start | bytes 811016 | tf_op jit(solution)/shard_map/ppermute | solution.py:32
  14.3 7.7 %collective-permute-start.5 = (bf16[32,4224]{1,0:T(8,128)(2,1)S(1)}, bf16[32,4224]{1,0:T(8,128)(2,1)S(1)}, u32[]{:S(2)}, u32[]{:S(2)}) collective-permute-start(bf16[32,4224]{1,0:T(8,128)(2,1)S(1)} %pad_maximum_fusion), channel_id=1, source_target_pairs={{0,8},{1,33},{2,10},{3,35},{4,12},{5,37},{6,14},{7,39},{8,16},{9,4... | collective-permute-start | bytes 811016 | tf_op jit(solution)/shard_map/ppermute | solution.py:32
  15.0 7.3 %collective-permute-start.3 = (bf16[32,4224]{1,0:T(8,128)(2,1)S(1)}, bf16[32,4224]{1,0:T(8,128)(2,1)S(1)}, u32[]{:S(2)}, u32[]{:S(2)}) collective-permute-start(bf16[32,4224]{1,0:T(8,128)(2,1)S(1)} %pad_maximum_fusion), channel_id=1, source_target_pairs={{0,24},{1,97},{2,26},{3,99},{4,28},{5,101},{6,30},{7,103},{8,0},{9... | collective-permute-start | bytes 811016 | tf_op jit(solution)/shard_map/ppermute | solution.py:32
  22.0 12.2 %collective-permute-start.7 = (bf16[64,4224]{1,0:T(8,128)(2,1)S(1)}, bf16[64,4224]{1,0:T(8,128)(2,1)S(1)}, u32[]{:S(2)}, u32[]{:S(2)}) collective-permute-start(bf16[64,4224]{1,0:T(8,128)(2,1)S(1)} %constant_dynamic-update-slice_fusion.5.refs_1_), channel_id=1, source_target_pairs={{0,1},{1,0},{2,3},{3,2},{4,5},{5,4},{6,7},{7,6},{8,9},{9,8},{10,11... | collective-permute-start | bytes 1622024 | tf_op jit(solution)/shard_map/ppermute | solution.py:36
  22.3 11.8 %collective-permute-start.6 = (bf16[64,4224]{1,0:T(8,128)(2,1)S(1)}, bf16[64,4224]{1,0:T(8,128)(2,1)S(1)}, u32[]{:S(2)}, u32[]{:S(2)}) collective-permute-start(bf16[64,4224]{1,0:T(8,128)(2,1)S(1)} %constant_dynamic-update-slice_fusion.refs_0_), channel_id=1, source_target_pairs={{0,1},{1,0},{2,3},{3,2},{4,5},{5,4},{6,7},{7,6},{8,9},{9,8},{10,11... | collective-permute-start | bytes 1622024 | tf_op jit(solution)/shard_map/ppermute | solution.py:36
  22.7 16.6 %collective-permute-start.10 = (bf16[64,4224]{1,0:T(8,128)(2,1)S(1)}, bf16[64,4224]{1,0:T(8,128)(2,1)S(1)}, u32[]{:S(2)}, u32[]{:S(2)}) collective-permute-start(bf16[64,4224]{1,0:T(8,128)(2,1)S(1)} %constant_dynamic-update-slice_fusion.5.refs_1_), channel_id=1, source_target_pairs={{0,32},{1,3},{2,34},{3,5},{4,36},{5,7},{6,38},{7,1},{8,40},{9,11},... | collective-permute-start | bytes 1622024 | tf_op jit(solution)/shard_map/ppermute | solution.py:32
  24.6 14.7 %collective-permute-start.9 = (bf16[64,4224]{1,0:T(8,128)(2,1)S(1)}, bf16[64,4224]{1,0:T(8,128)(2,1)S(1)}, u32[]{:S(2)}, u32[]{:S(2)}) collective-permute-start(bf16[64,4224]{1,0:T(8,128)(2,1)S(1)} %constant_dynamic-update-slice_fusion.refs_0_), channel_id=1, source_target_pairs={{0,96},{1,7},{2,98},{3,1},{4,100},{5,3},{6,102},{7,5},{8,104},{9,1... | collective-permute-start | bytes 1622024 | tf_op jit(solution)/shard_map/ppermute | solution.py:32
  39.3 3.1 %collective-permute-start.11 = (bf16[64,4224]{1,0:T(8,128)(2,1)S(1)}, bf16[64,4224]{1,0:T(8,128)(2,1)S(1)}, u32[]{:S(2)}, u32[]{:S(2)}) collective-permute-start(bf16[64,4224]{1,0:T(8,128)(2,1)S(1)} %collective-permute-done.9.refs_0_), channel_id=1, source_target_pairs={{0,1},{1,0},{2,3},{3,2},{4,5},{5,4},{6,7},{7,6},{8,9},{9,8},{10,11... | collective-permute-start | bytes 1622024 | tf_op jit(solution)/shard_map/ppermute | solution.py:36
  39.4 3.0 %collective-permute-start.12 = (bf16[64,4224]{1,0:T(8,128)(2,1)S(1)}, bf16[64,4224]{1,0:T(8,128)(2,1)S(1)}, u32[]{:S(2)}, u32[]{:S(2)}) collective-permute-start(bf16[64,4224]{1,0:T(8,128)(2,1)S(1)} %collective-permute-done.10.refs_1_), channel_id=1, source_target_pairs={{0,1},{1,0},{2,3},{3,2},{4,5},{5,4},{6,7},{7,6},{8,9},{9,8},{10,11... | collective-permute-start | bytes 1622024 | tf_op jit(solution)/shard_map/ppermute | solution.py:36
  39.9 9.4 %collective-permute-start.17 = (bf16[64,4224]{1,0:T(8,128)(2,1)S(1)}, bf16[64,4224]{1,0:T(8,128)(2,1)S(1)}, u32[]{:S(2)}, u32[]{:S(2)}) collective-permute-start(bf16[64,4224]{1,0:T(8,128)(2,1)S(1)} %collective-permute-done.9.refs_0_), channel_id=1, source_target_pairs={{0,96},{1,7},{2,98},{3,1},{4,100},{5,3},{6,102},{7,5},{8,104},{9,1... | collective-permute-start | bytes 1622024 | tf_op jit(solution)/shard_map/ppermute | solution.py:32
  42.4 10.6 %collective-permute-start.18 = (bf16[64,4224]{1,0:T(8,128)(2,1)S(1)}, bf16[64,4224]{1,0:T(8,128)(2,1)S(1)}, u32[]{:S(2)}, u32[]{:S(2)}) collective-permute-start(bf16[64,4224]{1,0:T(8,128)(2,1)S(1)} %collective-permute-done.10.refs_1_), channel_id=1, source_target_pairs={{0,32},{1,3},{2,34},{3,5},{4,36},{5,7},{6,38},{7,1},{8,40},{9,11},... | collective-permute-start | bytes 1622024 | tf_op jit(solution)/shard_map/ppermute | solution.py:32
  47.5 17.0 %collective-permute-start.13 = (bf16[128,4096]{1,0:T(8,128)(2,1)S(1)}, bf16[128,4096]{1,0:T(8,128)(2,1)S(1)}, u32[]{:S(2)}, u32[]{:S(2)}) collective-permute-start(bf16[128,4096]{1,0:T(8,128)(2,1)S(1)} %get-tuple-element.30), channel_id=1, source_target_pairs={{0,1},{1,0},{2,3},{3,2},{4,5},{5,4},{6,7},{7,6},{8,9},{9,8},{10,11... | collective-permute-start | bytes 3145736 | tf_op jit(solution)/shard_map/ppermute | solution.py:36
  53.5 9.4 %collective-permute-start.15 = (bf16[64,4224]{1,0:T(8,128)(2,1)S(1)}, bf16[64,4224]{1,0:T(8,128)(2,1)S(1)}, u32[]{:S(2)}, u32[]{:S(2)}) collective-permute-start(bf16[64,4224]{1,0:T(8,128)(2,1)S(1)} %constant_dynamic-update-slice_fusion.5.refs_1_), channel_id=1, source_target_pairs={{0,96},{1,7},{2,98},{3,1},{4,100},{5,3},{6,102},{7,5},{8,104},{9,1... | collective-permute-start | bytes 1622024 | tf_op jit(solution)/shard_map/ppermute | solution.py:32
  53.5 10.6 %collective-permute-start.16 = (bf16[64,4224]{1,0:T(8,128)(2,1)S(1)}, bf16[64,4224]{1,0:T(8,128)(2,1)S(1)}, u32[]{:S(2)}, u32[]{:S(2)}) collective-permute-start(bf16[64,4224]{1,0:T(8,128)(2,1)S(1)} %constant_dynamic-update-slice_fusion.refs_0_), channel_id=1, source_target_pairs={{0,32},{1,3},{2,34},{3,5},{4,36},{5,7},{6,38},{7,1},{8,40},{9,11},... | collective-permute-start | bytes 1622024 | tf_op jit(solution)/shard_map/ppermute | solution.py:32
  55.5 33.4 %collective-permute-start.8 = (bf16[128,4096]{1,0:T(8,128)(2,1)S(1)}, bf16[128,4096]{1,0:T(8,128)(2,1)S(1)}, u32[]{:S(2)}, u32[]{:S(2)}) collective-permute-start(bf16[128,4096]{1,0:T(8,128)(2,1)S(1)} %get-tuple-element.26), channel_id=1, source_target_pairs={{0,1},{1,0},{2,3},{3,2},{4,5},{5,4},{6,7},{7,6},{8,9},{9,8},{10,11... | collective-permute-start | bytes 3145736 | tf_op jit(solution)/shard_map/ppermute | solution.py:36
  60.8 12.7 %collective-permute-start.24 = (bf16[128,4096]{1,0:T(8,128)(2,1)S(1)}, bf16[128,4096]{1,0:T(8,128)(2,1)S(1)}, u32[]{:S(2)}, u32[]{:S(2)}) collective-permute-start(bf16[128,4096]{1,0:T(8,128)(2,1)S(1)} %get-tuple-element.35), channel_id=1, source_target_pairs={{0,1},{1,0},{2,3},{3,2},{4,5},{5,4},{6,7},{7,6},{8,9},{9,8},{10,11... | collective-permute-start | bytes 3145736 | tf_op jit(solution)/shard_map/ppermute | solution.py:36
  64.1 4.2 %collective-permute-start.22 = (bf16[64,4224]{1,0:T(8,128)(2,1)S(1)}, bf16[64,4224]{1,0:T(8,128)(2,1)S(1)}, u32[]{:S(2)}, u32[]{:S(2)}) collective-permute-start(bf16[64,4224]{1,0:T(8,128)(2,1)S(1)} %collective-permute-done.16.refs_1_), channel_id=1, source_target_pairs={{0,1},{1,0},{2,3},{3,2},{4,5},{5,4},{6,7},{7,6},{8,9},{9,8},{10,11... | collective-permute-start | bytes 1622024 | tf_op jit(solution)/shard_map/ppermute | solution.py:36
  64.9 24.2 %collective-permute-start.14 = (bf16[64,4096]{1,0:T(8,128)(2,1)S(1)}, bf16[64,4096]{1,0:T(8,128)(2,1)S(1)}, u32[]{:S(2)}, u32[]{:S(2)}) collective-permute-start(bf16[64,4096]{1,0:T(8,128)(2,1)S(1)} %get-tuple-element.44), channel_id=1, source_target_pairs={{0,32},{1,3},{2,34},{3,5},{4,36},{5,7},{6,38},{7,1},{8,40},{9,11},... | collective-permute-start | bytes 1572872 | tf_op jit(solution)/shard_map/ppermute | solution.py:32
  66.0 23.1 %collective-permute-start.28 = (bf16[64,4096]{1,0:T(8,128)(2,1)S(1)}, bf16[64,4096]{1,0:T(8,128)(2,1)S(1)}, u32[]{:S(2)}, u32[]{:S(2)}) collective-permute-start(bf16[64,4096]{1,0:T(8,128)(2,1)S(1)} %get-tuple-element.45), channel_id=1, source_target_pairs={{0,96},{1,7},{2,98},{3,1},{4,100},{5,3},{6,102},{7,5},{8,104},{9,1... | collective-permute-start | bytes 1572872 | tf_op jit(solution)/shard_map/ppermute | solution.py:32
  73.8 9.3 %collective-permute-start.25 = (bf16[64,4096]{1,0:T(8,128)(2,1)S(1)}, bf16[64,4096]{1,0:T(8,128)(2,1)S(1)}, u32[]{:S(2)}, u32[]{:S(2)}) collective-permute-start(bf16[64,4096]{1,0:T(8,128)(2,1)S(1)} %get-tuple-element.48), channel_id=1, source_target_pairs={{0,96},{1,7},{2,98},{3,1},{4,100},{5,3},{6,102},{7,5},{8,104},{9,1... | collective-permute-start | bytes 1572872 | tf_op jit(solution)/shard_map/ppermute | solution.py:32
  76.1 10.4 %collective-permute-start.29 = (bf16[64,4096]{1,0:T(8,128)(2,1)S(1)}, bf16[64,4096]{1,0:T(8,128)(2,1)S(1)}, u32[]{:S(2)}, u32[]{:S(2)}) collective-permute-start(bf16[64,4096]{1,0:T(8,128)(2,1)S(1)} %get-tuple-element.49), channel_id=1, source_target_pairs={{0,32},{1,3},{2,34},{3,5},{4,36},{5,7},{6,38},{7,1},{8,40},{9,11},... | collective-permute-start | bytes 1572872 | tf_op jit(solution)/shard_map/ppermute | solution.py:32
  86.8 9.3 %collective-permute-start.26 = (bf16[64,4096]{1,0:T(8,128)(2,1)S(1)}, bf16[64,4096]{1,0:T(8,128)(2,1)S(1)}, u32[]{:S(2)}, u32[]{:S(2)}) collective-permute-start(bf16[64,4096]{1,0:T(8,128)(2,1)S(1)} %get-tuple-element.46), channel_id=1, source_target_pairs={{0,96},{1,7},{2,98},{3,1},{4,100},{5,3},{6,102},{7,5},{8,104},{9,1... | collective-permute-start | bytes 1572872 | tf_op jit(solution)/shard_map/ppermute | solution.py:32
  86.9 10.5 %collective-permute-start.30 = (bf16[64,4096]{1,0:T(8,128)(2,1)S(1)}, bf16[64,4096]{1,0:T(8,128)(2,1)S(1)}, u32[]{:S(2)}, u32[]{:S(2)}) collective-permute-start(bf16[64,4096]{1,0:T(8,128)(2,1)S(1)} %get-tuple-element.47), channel_id=1, source_target_pairs={{0,32},{1,3},{2,34},{3,5},{4,36},{5,7},{6,38},{7,1},{8,40},{9,11},... | collective-permute-start | bytes 1572872 | tf_op jit(solution)/shard_map/ppermute | solution.py:32
  97.6 7.7 %collective-permute-start.27 = (bf16[32,4096]{1,0:T(8,128)(2,1)S(1)}, bf16[32,4096]{1,0:T(8,128)(2,1)S(1)}, u32[]{:S(2)}, u32[]{:S(2)}) collective-permute-start(bf16[32,4096]{1,0:T(8,128)(2,1)S(1)} %get-tuple-element.43), channel_id=1, source_target_pairs={{0,8},{1,33},{2,10},{3,35},{4,12},{5,37},{6,14},{7,39},{8,16},{9,4... | collective-permute-start | bytes 786440 | tf_op jit(solution)/shard_map/ppermute | solution.py:32
  99.2 9.9 %collective-permute-start.31 = (bf16[32,4096]{1,0:T(8,128)(2,1)S(1)}, bf16[32,4096]{1,0:T(8,128)(2,1)S(1)}, u32[]{:S(2)}, u32[]{:S(2)}) collective-permute-start(bf16[32,4096]{1,0:T(8,128)(2,1)S(1)} %get-tuple-element.41), channel_id=1, source_target_pairs={{0,16},{1,65},{2,18},{3,67},{4,20},{5,69},{6,22},{7,71},{8,24},{9,... | collective-permute-start | bytes 786440 | tf_op jit(solution)/shard_map/ppermute | solution.py:32
  102.0 7.2 %collective-permute-start.32 = (bf16[32,4096]{1,0:T(8,128)(2,1)S(1)}, bf16[32,4096]{1,0:T(8,128)(2,1)S(1)}, u32[]{:S(2)}, u32[]{:S(2)}) collective-permute-start(bf16[32,4096]{1,0:T(8,128)(2,1)S(1)} %get-tuple-element.42), channel_id=1, source_target_pairs={{0,24},{1,97},{2,26},{3,99},{4,28},{5,101},{6,30},{7,103},{8,0},{9... | collective-permute-start | bytes 786440 | tf_op jit(solution)/shard_map/ppermute | solution.py:32
  109.4 6.2 %collective-permute-start.33 = (bf16[8,4096]{1,0:T(8,128)(2,1)S(1)}, bf16[8,4096]{1,0:T(8,128)(2,1)S(1)}, u32[]{:S(2)}, u32[]{:S(2)}) collective-permute-start(bf16[8,4096]{1,0:T(8,128)(2,1)S(1)} %get-tuple-element.50), channel_id=1, source_target_pairs={{0,2},{1,9},{2,4},{3,11},{4,6},{5,13},{6,0},{7,15},{8,10},{9,17},{... | collective-permute-start | bytes 196616 | tf_op jit(solution)/shard_map/ppermute | solution.py:32
  109.5 6.2 %collective-permute-start.34 = (bf16[8,4096]{1,0:T(8,128)(2,1)S(1)}, bf16[8,4096]{1,0:T(8,128)(2,1)S(1)}, u32[]{:S(2)}, u32[]{:S(2)}) collective-permute-start(bf16[8,4096]{1,0:T(8,128)(2,1)S(1)} %get-tuple-element.52), channel_id=1, source_target_pairs={{0,4},{1,17},{2,6},{3,19},{4,0},{5,21},{6,2},{7,23},{8,12},{9,25},... | collective-permute-start | bytes 196616 | tf_op jit(solution)/shard_map/ppermute | solution.py:32
  111.2 5.3 %collective-permute-start.35 = (bf16[8,4096]{1,0:T(8,128)(2,1)S(1)}, bf16[8,4096]{1,0:T(8,128)(2,1)S(1)}, u32[]{:S(2)}, u32[]{:S(2)}) collective-permute-start(bf16[8,4096]{1,0:T(8,128)(2,1)S(1)} %get-tuple-element.51), channel_id=1, source_target_pairs={{0,6},{1,25},{2,0},{3,27},{4,2},{5,29},{6,4},{7,31},{8,14},{9,1},{... | collective-permute-start | bytes 196616 | tf_op jit(solution)/shard_map/ppermute | solution.py:32
  (4 other events, 9.9 us)

commit v2 on v1

--- a/solution.py
+++ b/solution.py
@@ -150,23 +150,23 @@
     behind_b = move(near_b, 1)
 
     own0, other0 = experts((near_a, near_b, swap(near_a), swap(near_b)), *weights)
-    ahead_a, behind_b, near_a, near_b = after((ahead_a, behind_b, near_a, near_b), other0)
+    ahead_a, behind_b = after((ahead_a, behind_b), other0)
     far_a = move(ahead_a, -1)
     far_b = move(behind_b, 1)
     ahead_b = move(near_b, -1)
     behind_a = move(near_a, 1)
     pieces = (ahead_a, behind_b, swap(ahead_a), swap(behind_b))
     own1, other1 = experts(pieces, *weights)
-    sum1 = added(own1, swap(other1))
+    back1 = swap(other1)
 
     far_a, far_b = after((far_a, far_b), other1)
     pieces = (far_a, far_b, swap(far_a), swap(far_b))
     own2, other2 = experts(pieces, *weights)
-    sum2 = added(own2, swap(other2))
-    through_a = move(sum2[:half], -1)
-    through_b = move(sum2[half:], 1)
-    got_a = move(sum1[:half], 1)
-    got_b = move(sum1[half:], -1)
+    back2 = swap(other2)
+    through_a = move(added(own2[:half], back2[:half]), -1)
+    through_b = move(added(own2[half:], back2[half:]), 1)
+    got_a = move(added(own1[:half], back1[:half]), 1)
+    got_b = move(added(own1[half:], back1[half:]), -1)
 
     ahead_b, behind_a = after((ahead_b, behind_a), other2)
     pieces = (ahead_b, behind_a, swap(ahead_b), swap(behind_a))

time: 117 us -> 123 us (1.051)
  starting transfers between devices: 35.8 us -> 40 us
    ppermute x24, starting transfers between devices: 33.2 us -> 37.3 us  [move(): return lax.ppermute(value, AXES, pairs(phase, step))]
    ppermute x24, waiting for transfers between devices: 46.3 us -> 48.2 us  [move(): return lax.ppermute(value, AXES, pairs(phase, step))]
  transfers between devices with their start and end apart: 36 -> 36, of which waited for: 21 -> 21; matrix products, arithmetic and copies ran while one was open for 1% -> 1% of each run, Pallas kernels for 24% -> 23%
where the time goes in v2:
time: 123 us; the launch traced here: 122 us
  waiting for transfers between devices  50.1 us (41%)
  starting transfers between devices  40 us (33%)
  Pallas kernels  27.7 us (23%)
  other arithmetic  3.12 us (3%)
    ppermute x24, waiting for transfers between devices, move(): return lax.ppermute(value, AXES, pairs(phase, step))  48.2 us
    ppermute x24, starting transfers between devices, move(): return lax.ppermute(value, AXES, pairs(phase, step))  37.3 us
    pallas_call x4, Pallas kernels, experts(): pl.pallas_call(functools.partial(expert_kernel, counts, local, width, hid...  20.3 us
    pallas_call x2, Pallas kernels, loaded(): pl.pallas_call(functools.partial(load_kernel, count), out_shape=[pltpu.VM...  7.42 us
    ppermute x12, starting transfers between devices, swap(): return lax.ppermute(value, AXES, [(i, i ^ 1) for i in range(128)])  2.78 us
  transfers between devices with their start and end apart: 36, of which 21 were waited for; matrix products, arithmetic and copies ran while one was open for 1% of the time, Pallas kernels for 23%

profile of v2, /device:TPU:0, one launch (start us, length us, event | category | flops | bytes accessed | tf_op | source)
XLA Modules:
  0.0 122.2 jit_solution(1776890946063413040)
XLA Ops:
  1.6 2.9 %collective-permute-start = (bf16[8,4224]{1,0:T(8,128)(2,1)S(1)}, bf16[8,4224]{1,0:T(8,128)(2,1)S(1)}, u32[]{:S(2)}, u32[]{:S(2)}) collective-permute-start(bf16[8,4224]{1,0:T(8,128)(2,1)S(1)} %concatenate.13), channel_id=1, source_target_pairs={{0,6},{1,25},{2,0},{3,27},{4,2},{5,29},{6,4},{7,31},{8,14},{9,1},{... | collective-permute-start | bytes 202760 | tf_op jit(solution)/shard_map/ppermute | solution.py:32
  6.4 3.9 %collective-permute-done.1 = bf16[8,4224]{1,0:T(8,128)(2,1)S(1)} collective-permute-done((bf16[8,4224]{1,0:T(8,128)(2,1)S(1)}, bf16[8,4224]{1,0:T(8,128)(2,1)S(1)}, u32[]{:S(2)}, u32[]{:S(2)}) %collective-permute-start.1) | collective-permute-done | bytes 67616 | tf_op jit(solution)/shard_map/ppermute | solution.py:32
  11.0 3.3 %collective-permute-start.4 = (bf16[32,4224]{1,0:T(8,128)(2,1)S(1)}, bf16[32,4224]{1,0:T(8,128)(2,1)S(1)}, u32[]{:S(2)}, u32[]{:S(2)}) collective-permute-start(bf16[32,4224]{1,0:T(8,128)(2,1)S(1)} %pad_maximum_fusion), channel_id=1, source_target_pairs={{0,16},{1,65},{2,18},{3,67},{4,20},{5,69},{6,22},{7,71},{8,24},{9,... | collective-permute-start | bytes 811016 | tf_op jit(solution)/shard_map/ppermute | solution.py:32
  15.0 2.6 %collective-permute-start.3 = (bf16[32,4224]{1,0:T(8,128)(2,1)S(1)}, bf16[32,4224]{1,0:T(8,128)(2,1)S(1)}, u32[]{:S(2)}, u32[]{:S(2)}) collective-permute-start(bf16[32,4224]{1,0:T(8,128)(2,1)S(1)} %pad_maximum_fusion), channel_id=1, source_target_pairs={{0,24},{1,97},{2,26},{3,99},{4,28},{5,101},{6,30},{7,103},{8,0},{9... | collective-permute-start | bytes 811016 | tf_op jit(solution)/shard_map/ppermute | solution.py:32
  17.6 1.5 %collective-permute-done.4 = bf16[32,4224]{1,0:T(8,128)(2,1)S(1)} collective-permute-done((bf16[32,4224]{1,0:T(8,128)(2,1)S(1)}, bf16[32,4224]{1,0:T(8,128)(2,1)S(1)}, u32[]{:S(2)}, u32[]{:S(2)}) %collective-permute-start.4) | collective-permute-done | bytes 270368 | tf_op jit(solution)/shard_map/ppermute | solution.py:32
  19.1 2.9 %collective-permute-done.5 = bf16[32,4224]{1,0:T(8,128)(2,1)S(1)} collective-permute-done((bf16[32,4224]{1,0:T(8,128)(2,1)S(1)}, bf16[32,4224]{1,0:T(8,128)(2,1)S(1)}, u32[]{:S(2)}, u32[]{:S(2)}) %collective-permute-start.5) | collective-permute-done | bytes 270368 | tf_op jit(solution)/shard_map/ppermute | solution.py:32
  22.7 1.9 %collective-permute-start.10 = (bf16[64,4224]{1,0:T(8,128)(2,1)S(1)}, bf16[64,4224]{1,0:T(8,128)(2,1)S(1)}, u32[]{:S(2)}, u32[]{:S(2)}) collective-permute-start(bf16[64,4224]{1,0:T(8,128)(2,1)S(1)} %constant_dynamic-update-slice_fusion.5.refs_1_), channel_id=1, source_target_pairs={{0,32},{1,3},{2,34},{3,5},{4,36},{5,7},{6,38},{7,1},{8,40},{9,11},... | collective-permute-start | bytes 1622024 | tf_op jit(solution)/shard_map/ppermute | solution.py:32
  24.6 2.1 %collective-permute-start.9 = (bf16[64,4224]{1,0:T(8,128)(2,1)S(1)}, bf16[64,4224]{1,0:T(8,128)(2,1)S(1)}, u32[]{:S(2)}, u32[]{:S(2)}) collective-permute-start(bf16[64,4224]{1,0:T(8,128)(2,1)S(1)} %constant_dynamic-update-slice_fusion.refs_0_), channel_id=1, source_target_pairs={{0,96},{1,7},{2,98},{3,1},{4,100},{5,3},{6,102},{7,5},{8,104},{9,1... | collective-permute-start | bytes 1622024 | tf_op jit(solution)/shard_map/ppermute | solution.py:32
  26.7 2.8 %shard_map.64.refs_4_ = bf16[2,4096,384]{2,1,0:T(8,128)(2,1)S(1)} custom-call(bf16[2,4096,384]{2,1,0:T(8,128)(2,1)} %refs_0_.2), custom_call_target="tpu_custom_call" | custom-call | bytes 16000000 | tf_op jit(solution)/shard_map/pallas_call | solution.py:57
  29.5 4.6 %shard_map.65 = (bf16[2,4096,384]{2,1,0:T(8,128)(2,1)S(1)}, bf16[768,4096]{1,0:T(8,128)(2,1)S(1)}) custom-call(bf16[2,4096,384]{2,1,0:T(8,128)(2,1)} %refs_0_.3, bf16[768,4096]{1,0:T(8,128)(2,1)} %bitcast.1), custom_call_target="tpu_custom_call" | custom-call | bytes 16000000 | tf_op jit(solution)/shard_map/pallas_call | solution.py:57
  34.2 5.1 %shard_map.66 = (bf16[128,4096]{1,0:T(8,128)(2,1)S(1)}, bf16[128,4096]{1,0:T(8,128)(2,1)S(1)}) custom-call(bf16[64,4224]{1,0:T(8,128)(2,1)S(1)} %constant_dynamic-update-slice_fusion.refs_0_, bf16[64,4224]{1,0:T(8,128)(2,1)S(1)} %constant_dynamic-update-slice_fusion.5.refs_1_, bf16[64,4224]{1,0:T(8,128)(2,1)S(1)} %collective-permute-done.6.refs_2_, ...), custom_call_target="tpu_custom_call" | custom-call | flops 4831838208 | bytes 4194304 | tf_op jit(solution)/shard_map/pallas_call | solution.py:112
  39.9 2.5 %collective-permute-start.17 = (bf16[64,4224]{1,0:T(8,128)(2,1)S(1)}, bf16[64,4224]{1,0:T(8,128)(2,1)S(1)}, u32[]{:S(2)}, u32[]{:S(2)}) collective-permute-start(bf16[64,4224]{1,0:T(8,128)(2,1)S(1)} %collective-permute-done.9.refs_0_), channel_id=1, source_target_pairs={{0,96},{1,7},{2,98},{3,1},{4,100},{5,3},{6,102},{7,5},{8,104},{9,1... | collective-permute-start | bytes 1622024 | tf_op jit(solution)/shard_map/ppermute | solution.py:32
  42.4 5.1 %shard_map.67 = (bf16[128,4096]{1,0:T(8,128)(2,1)S(1)}, bf16[128,4096]{1,0:T(8,128)(2,1)S(1)}) custom-call(bf16[64,4224]{1,0:T(8,128)(2,1)S(1)} %collective-permute-done.9.refs_0_, bf16[64,4224]{1,0:T(8,128)(2,1)S(1)} %collective-permute-done.10.refs_1_, bf16[64,4224]{1,0:T(8,128)(2,1)S(1)} %collective-permute-done.11.refs_2_, ...), custom_call_target="tpu_custom_call" | custom-call | flops 4831838208 | bytes 4194304 | tf_op jit(solution)/shard_map/pallas_call | solution.py:112
  47.5 1.8 %collective-permute-done.17.refs_0_ = bf16[64,4224]{1,0:T(8,128)(2,1)S(1)} collective-permute-done((bf16[64,4224]{1,0:T(8,128)(2,1)S(1)}, bf16[64,4224]{1,0:T(8,128)(2,1)S(1)}, u32[]{:S(2)}, u32[]{:S(2)}) %collective-permute-start.17) | collective-permute-done | bytes 540704 | tf_op jit(solution)/shard_map/ppermute | solution.py:32
  49.3 3.7 %collective-permute-done.18.refs_1_ = bf16[64,4224]{1,0:T(8,128)(2,1)S(1)} collective-permute-done((bf16[64,4224]{1,0:T(8,128)(2,1)S(1)}, bf16[64,4224]{1,0:T(8,128)(2,1)S(1)}, u32[]{:S(2)}, u32[]{:S(2)}) %collective-permute-start.18) | collective-permute-done | bytes 540704 | tf_op jit(solution)/shard_map/ppermute | solution.py:32
  53.5 2.0 %collective-permute-start.16 = (bf16[64,4224]{1,0:T(8,128)(2,1)S(1)}, bf16[64,4224]{1,0:T(8,128)(2,1)S(1)}, u32[]{:S(2)}, u32[]{:S(2)}) collective-permute-start(bf16[64,4224]{1,0:T(8,128)(2,1)S(1)} %constant_dynamic-update-slice_fusion.refs_0_), channel_id=1, source_target_pairs={{0,32},{1,3},{2,34},{3,5},{4,36},{5,7},{6,38},{7,1},{8,40},{9,11},... | collective-permute-start | bytes 1622024 | tf_op jit(solution)/shard_map/ppermute | solution.py:32
  55.7 5.1 %shard_map.68 = (bf16[128,4096]{1,0:T(8,128)(2,1)S(1)}, bf16[128,4096]{1,0:T(8,128)(2,1)S(1)}) custom-call(bf16[64,4224]{1,0:T(8,128)(2,1)S(1)} %collective-permute-done.17.refs_0_, bf16[64,4224]{1,0:T(8,128)(2,1)S(1)} %collective-permute-done.18.refs_1_, bf16[64,4224]{1,0:T(8,128)(2,1)S(1)} %collective-permute-done.19.refs_2_, ...), custom_call_target="tpu_custom_call" | custom-call | flops 4831838208 | bytes 4194304 | tf_op jit(solution)/shard_map/pallas_call | solution.py:112
  60.7 2.1 %collective-permute-done.15.refs_0_ = bf16[64,4224]{1,0:T(8,128)(2,1)S(1)} collective-permute-done((bf16[64,4224]{1,0:T(8,128)(2,1)S(1)}, bf16[64,4224]{1,0:T(8,128)(2,1)S(1)}, u32[]{:S(2)}, u32[]{:S(2)}) %collective-permute-start.15) | collective-permute-done | bytes 540704 | tf_op jit(solution)/shard_map/ppermute | solution.py:32
  66.7 5.1 %shard_map.69 = (bf16[128,4096]{1,0:T(8,128)(2,1)S(1)}, bf16[128,4096]{1,0:T(8,128)(2,1)S(1)}) custom-call(bf16[64,4224]{1,0:T(8,128)(2,1)S(1)} %collective-permute-done.15.refs_0_, bf16[64,4224]{1,0:T(8,128)(2,1)S(1)} %collective-permute-done.16.refs_1_, bf16[64,4224]{1,0:T(8,128)(2,1)S(1)} %collective-permute-done.21.refs_2_, ...), custom_call_target="tpu_custom_call" | custom-call | flops 4831838208 | bytes 4194304 | tf_op jit(solution)/shard_map/pallas_call | solution.py:112
  73.2 2.4 %collective-permute-start.28 = (bf16[64,4096]{1,0:T(8,128)(2,1)S(1)}, bf16[64,4096]{1,0:T(8,128)(2,1)S(1)}, u32[]{:S(2)}, u32[]{:S(2)}) collective-permute-start(bf16[64,4096]{1,0:T(8,128)(2,1)S(1)} %get-tuple-element.38), channel_id=1, source_target_pairs={{0,96},{1,7},{2,98},{3,1},{4,100},{5,3},{6,102},{7,5},{8,104},{9,1... | collective-permute-start | bytes 1572872 | tf_op jit(solution)/shard_map/ppermute | solution.py:32
  76.0 2.0 %collective-permute-start.29 = (bf16[64,4096]{1,0:T(8,128)(2,1)S(1)}, bf16[64,4096]{1,0:T(8,128)(2,1)S(1)}, u32[]{:S(2)}, u32[]{:S(2)}) collective-permute-start(bf16[64,4096]{1,0:T(8,128)(2,1)S(1)} %get-tuple-element.40), channel_id=1, source_target_pairs={{0,32},{1,3},{2,34},{3,5},{4,36},{5,7},{6,38},{7,1},{8,40},{9,11},... | collective-permute-start | bytes 1572872 | tf_op jit(solution)/shard_map/ppermute | solution.py:32
  78.2 9.8 %collective-permute-done.25 = bf16[64,4096]{1,0:T(8,128)(2,1)S(1)} collective-permute-done((bf16[64,4096]{1,0:T(8,128)(2,1)S(1)}, bf16[64,4096]{1,0:T(8,128)(2,1)S(1)}, u32[]{:S(2)}, u32[]{:S(2)}) %collective-permute-start.25) | collective-permute-done | bytes 524320 | tf_op jit(solution)/shard_map/ppermute | solution.py:32
  88.6 3.3 %collective-permute-start.26 = (bf16[64,4096]{1,0:T(8,128)(2,1)S(1)}, bf16[64,4096]{1,0:T(8,128)(2,1)S(1)}, u32[]{:S(2)}, u32[]{:S(2)}) collective-permute-start(bf16[64,4096]{1,0:T(8,128)(2,1)S(1)} %get-tuple-element.44), channel_id=1, source_target_pairs={{0,96},{1,7},{2,98},{3,1},{4,100},{5,3},{6,102},{7,5},{8,104},{9,1... | collective-permute-start | bytes 1572872 | tf_op jit(solution)/shard_map/ppermute | solution.py:32
  92.2 6.4 %collective-permute-done.26 = bf16[64,4096]{1,0:T(8,128)(2,1)S(1)} collective-permute-done((bf16[64,4096]{1,0:T(8,128)(2,1)S(1)}, bf16[64,4096]{1,0:T(8,128)(2,1)S(1)}, u32[]{:S(2)}, u32[]{:S(2)}) %collective-permute-start.26) | collective-permute-done | bytes 524320 | tf_op jit(solution)/shard_map/ppermute | solution.py:32
  98.6 3.7 %collective-permute-done.30 = bf16[64,4096]{1,0:T(8,128)(2,1)S(1)} collective-permute-done((bf16[64,4096]{1,0:T(8,128)(2,1)S(1)}, bf16[64,4096]{1,0:T(8,128)(2,1)S(1)}, u32[]{:S(2)}, u32[]{:S(2)}) %collective-permute-start.30) | collective-permute-done | bytes 524320 | tf_op jit(solution)/shard_map/ppermute | solution.py:32
  102.6 1.6 %collective-permute-start.27 = (bf16[32,4096]{1,0:T(8,128)(2,1)S(1)}, bf16[32,4096]{1,0:T(8,128)(2,1)S(1)}, u32[]{:S(2)}, u32[]{:S(2)}) collective-permute-start(bf16[32,4096]{1,0:T(8,128)(2,1)S(1)} %get-tuple-element.43), channel_id=1, source_target_pairs={{0,8},{1,33},{2,10},{3,35},{4,12},{5,37},{6,14},{7,39},{8,16},{9,4... | collective-permute-start | bytes 786440 | tf_op jit(solution)/shard_map/ppermute | solution.py:32
  104.3 2.8 %collective-permute-start.31 = (bf16[32,4096]{1,0:T(8,128)(2,1)S(1)}, bf16[32,4096]{1,0:T(8,128)(2,1)S(1)}, u32[]{:S(2)}, u32[]{:S(2)}) collective-permute-start(bf16[32,4096]{1,0:T(8,128)(2,1)S(1)} %get-tuple-element.41), channel_id=1, source_target_pairs={{0,16},{1,65},{2,18},{3,67},{4,20},{5,69},{6,22},{7,71},{8,24},{9,... | collective-permute-start | bytes 786440 | tf_op jit(solution)/shard_map/ppermute | solution.py:32
  107.6 2.7 %collective-permute-done.27 = bf16[32,4096]{1,0:T(8,128)(2,1)S(1)} collective-permute-done((bf16[32,4096]{1,0:T(8,128)(2,1)S(1)}, bf16[32,4096]{1,0:T(8,128)(2,1)S(1)}, u32[]{:S(2)}, u32[]{:S(2)}) %collective-permute-start.27) | collective-permute-done | bytes 262176 | tf_op jit(solution)/shard_map/ppermute | solution.py:32
  110.3 3.9 %collective-permute-done.31 = bf16[32,4096]{1,0:T(8,128)(2,1)S(1)} collective-permute-done((bf16[32,4096]{1,0:T(8,128)(2,1)S(1)}, bf16[32,4096]{1,0:T(8,128)(2,1)S(1)}, u32[]{:S(2)}, u32[]{:S(2)}) %collective-permute-start.31) | collective-permute-done | bytes 262176 | tf_op jit(solution)/shard_map/ppermute | solution.py:32
  114.5 1.7 %collective-permute-start.34 = (bf16[8,4096]{1,0:T(8,128)(2,1)S(1)}, bf16[8,4096]{1,0:T(8,128)(2,1)S(1)}, u32[]{:S(2)}, u32[]{:S(2)}) collective-permute-start(bf16[8,4096]{1,0:T(8,128)(2,1)S(1)} %get-tuple-element.48), channel_id=1, source_target_pairs={{0,4},{1,17},{2,6},{3,19},{4,0},{5,21},{6,2},{7,23},{8,12},{9,25},... | collective-permute-start | bytes 196616 | tf_op jit(solution)/shard_map/ppermute | solution.py:32
  116.3 2.2 %collective-permute-start.35 = (bf16[8,4096]{1,0:T(8,128)(2,1)S(1)}, bf16[8,4096]{1,0:T(8,128)(2,1)S(1)}, u32[]{:S(2)}, u32[]{:S(2)}) collective-permute-start(bf16[8,4096]{1,0:T(8,128)(2,1)S(1)} %get-tuple-element.47), channel_id=1, source_target_pairs={{0,6},{1,25},{2,0},{3,27},{4,2},{5,29},{6,4},{7,31},{8,14},{9,1},{... | collective-permute-start | bytes 196616 | tf_op jit(solution)/shard_map/ppermute | solution.py:32
  118.4 2.3 %collective-permute-done.33 = bf16[8,4096]{1,0:T(8,128)(2,1)S(1)} collective-permute-done((bf16[8,4096]{1,0:T(8,128)(2,1)S(1)}, bf16[8,4096]{1,0:T(8,128)(2,1)S(1)}, u32[]{:S(2)}, u32[]{:S(2)}) %collective-permute-start.33) | collective-permute-done | bytes 65568 | tf_op jit(solution)/shard_map/ppermute | solution.py:32
  (66 shorter events, 16.4 us)
Async XLA Ops:
  1.6 4.8 %collective-permute-start = (bf16[8,4224]{1,0:T(8,128)(2,1)S(1)}, bf16[8,4224]{1,0:T(8,128)(2,1)S(1)}, u32[]{:S(2)}, u32[]{:S(2)}) collective-permute-start(bf16[8,4224]{1,0:T(8,128)(2,1)S(1)} %concatenate.13), channel_id=1, source_target_pairs={{0,6},{1,25},{2,0},{3,27},{4,2},{5,29},{6,4},{7,31},{8,14},{9,1},{... | collective-permute-start | bytes 202760 | tf_op jit(solution)/shard_map/ppermute | solution.py:32
  4.5 5.8 %collective-permute-start.1 = (bf16[8,4224]{1,0:T(8,128)(2,1)S(1)}, bf16[8,4224]{1,0:T(8,128)(2,1)S(1)}, u32[]{:S(2)}, u32[]{:S(2)}) collective-permute-start(bf16[8,4224]{1,0:T(8,128)(2,1)S(1)} %concatenate.13), channel_id=1, source_target_pairs={{0,4},{1,17},{2,6},{3,19},{4,0},{5,21},{6,2},{7,23},{8,12},{9,25},... | collective-permute-start | bytes 202760 | tf_op jit(solution)/shard_map/ppermute | solution.py:32
  5.3 5.7 %collective-permute-start.2 = (bf16[8,4224]{1,0:T(8,128)(2,1)S(1)}, bf16[8,4224]{1,0:T(8,128)(2,1)S(1)}, u32[]{:S(2)}, u32[]{:S(2)}) collective-permute-start(bf16[8,4224]{1,0:T(8,128)(2,1)S(1)} %concatenate.13), channel_id=1, source_target_pairs={{0,2},{1,9},{2,4},{3,11},{4,6},{5,13},{6,0},{7,15},{8,10},{9,17},{... | collective-permute-start | bytes 202760 | tf_op jit(solution)/shard_map/ppermute | solution.py:32
  11.0 8.0 %collective-permute-start.4 = (bf16[32,4224]{1,0:T(8,128)(2,1)S(1)}, bf16[32,4224]{1,0:T(8,128)(2,1)S(1)}, u32[]{:S(2)}, u32[]{:S(2)}) collective-permute-start(bf16[32,4224]{1,0:T(8,128)(2,1)S(1)} %pad_maximum_fusion), channel_id=1, source_target_pairs={{0,16},{1,65},{2,18},{3,67},{4,20},{5,69},{6,22},{7,71},{8,24},{9,... | collective-permute-start | bytes 811016 | tf_op jit(solution)/shard_map/ppermute | solution.py:32
  14.3 7.7 %collective-permute-start.5 = (bf16[32,4224]{1,0:T(8,128)(2,1)S(1)}, bf16[32,4224]{1,0:T(8,128)(2,1)S(1)}, u32[]{:S(2)}, u32[]{:S(2)}) collective-permute-start(bf16[32,4224]{1,0:T(8,128)(2,1)S(1)} %pad_maximum_fusion), channel_id=1, source_target_pairs={{0,8},{1,33},{2,10},{3,35},{4,12},{5,37},{6,14},{7,39},{8,16},{9,4... | collective-permute-start | bytes 811016 | tf_op jit(solution)/shard_map/ppermute | solution.py:32
  15.0 7.3 %collective-permute-start.3 = (bf16[32,4224]{1,0:T(8,128)(2,1)S(1)}, bf16[32,4224]{1,0:T(8,128)(2,1)S(1)}, u32[]{:S(2)}, u32[]{:S(2)}) collective-permute-start(bf16[32,4224]{1,0:T(8,128)(2,1)S(1)} %pad_maximum_fusion), channel_id=1, source_target_pairs={{0,24},{1,97},{2,26},{3,99},{4,28},{5,101},{6,30},{7,103},{8,0},{9... | collective-permute-start | bytes 811016 | tf_op jit(solution)/shard_map/ppermute | solution.py:32
  22.0 12.2 %collective-permute-start.7 = (bf16[64,4224]{1,0:T(8,128)(2,1)S(1)}, bf16[64,4224]{1,0:T(8,128)(2,1)S(1)}, u32[]{:S(2)}, u32[]{:S(2)}) collective-permute-start(bf16[64,4224]{1,0:T(8,128)(2,1)S(1)} %constant_dynamic-update-slice_fusion.5.refs_1_), channel_id=1, source_target_pairs={{0,1},{1,0},{2,3},{3,2},{4,5},{5,4},{6,7},{7,6},{8,9},{9,8},{10,11... | collective-permute-start | bytes 1622024 | tf_op jit(solution)/shard_map/ppermute | solution.py:36
  22.3 11.8 %collective-permute-start.6 = (bf16[64,4224]{1,0:T(8,128)(2,1)S(1)}, bf16[64,4224]{1,0:T(8,128)(2,1)S(1)}, u32[]{:S(2)}, u32[]{:S(2)}) collective-permute-start(bf16[64,4224]{1,0:T(8,128)(2,1)S(1)} %constant_dynamic-update-slice_fusion.refs_0_), channel_id=1, source_target_pairs={{0,1},{1,0},{2,3},{3,2},{4,5},{5,4},{6,7},{7,6},{8,9},{9,8},{10,11... | collective-permute-start | bytes 1622024 | tf_op jit(solution)/shard_map/ppermute | solution.py:36
  22.7 16.6 %collective-permute-start.10 = (bf16[64,4224]{1,0:T(8,128)(2,1)S(1)}, bf16[64,4224]{1,0:T(8,128)(2,1)S(1)}, u32[]{:S(2)}, u32[]{:S(2)}) collective-permute-start(bf16[64,4224]{1,0:T(8,128)(2,1)S(1)} %constant_dynamic-update-slice_fusion.5.refs_1_), channel_id=1, source_target_pairs={{0,32},{1,3},{2,34},{3,5},{4,36},{5,7},{6,38},{7,1},{8,40},{9,11},... | collective-permute-start | bytes 1622024 | tf_op jit(solution)/shard_map/ppermute | solution.py:32
  24.6 14.7 %collective-permute-start.9 = (bf16[64,4224]{1,0:T(8,128)(2,1)S(1)}, bf16[64,4224]{1,0:T(8,128)(2,1)S(1)}, u32[]{:S(2)}, u32[]{:S(2)}) collective-permute-start(bf16[64,4224]{1,0:T(8,128)(2,1)S(1)} %constant_dynamic-update-slice_fusion.refs_0_), channel_id=1, source_target_pairs={{0,96},{1,7},{2,98},{3,1},{4,100},{5,3},{6,102},{7,5},{8,104},{9,1... | collective-permute-start | bytes 1622024 | tf_op jit(solution)/shard_map/ppermute | solution.py:32
  39.3 3.1 %collective-permute-start.11 = (bf16[64,4224]{1,0:T(8,128)(2,1)S(1)}, bf16[64,4224]{1,0:T(8,128)(2,1)S(1)}, u32[]{:S(2)}, u32[]{:S(2)}) collective-permute-start(bf16[64,4224]{1,0:T(8,128)(2,1)S(1)} %collective-permute-done.9.refs_0_), channel_id=1, source_target_pairs={{0,1},{1,0},{2,3},{3,2},{4,5},{5,4},{6,7},{7,6},{8,9},{9,8},{10,11... | collective-permute-start | bytes 1622024 | tf_op jit(solution)/shard_map/ppermute | solution.py:36
  39.4 3.0 %collective-permute-start.12 = (bf16[64,4224]{1,0:T(8,128)(2,1)S(1)}, bf16[64,4224]{1,0:T(8,128)(2,1)S(1)}, u32[]{:S(2)}, u32[]{:S(2)}) collective-permute-start(bf16[64,4224]{1,0:T(8,128)(2,1)S(1)} %collective-permute-done.10.refs_1_), channel_id=1, source_target_pairs={{0,1},{1,0},{2,3},{3,2},{4,5},{5,4},{6,7},{7,6},{8,9},{9,8},{10,11... | collective-permute-start | bytes 1622024 | tf_op jit(solution)/shard_map/ppermute | solution.py:36
  39.9 9.4 %collective-permute-start.17 = (bf16[64,4224]{1,0:T(8,128)(2,1)S(1)}, bf16[64,4224]{1,0:T(8,128)(2,1)S(1)}, u32[]{:S(2)}, u32[]{:S(2)}) collective-permute-start(bf16[64,4224]{1,0:T(8,128)(2,1)S(1)} %collective-permute-done.9.refs_0_), channel_id=1, source_target_pairs={{0,96},{1,7},{2,98},{3,1},{4,100},{5,3},{6,102},{7,5},{8,104},{9,1... | collective-permute-start | bytes 1622024 | tf_op jit(solution)/shard_map/ppermute | solution.py:32
  42.4 10.6 %collective-permute-start.18 = (bf16[64,4224]{1,0:T(8,128)(2,1)S(1)}, bf16[64,4224]{1,0:T(8,128)(2,1)S(1)}, u32[]{:S(2)}, u32[]{:S(2)}) collective-permute-start(bf16[64,4224]{1,0:T(8,128)(2,1)S(1)} %collective-permute-done.10.refs_1_), channel_id=1, source_target_pairs={{0,32},{1,3},{2,34},{3,5},{4,36},{5,7},{6,38},{7,1},{8,40},{9,11},... | collective-permute-start | bytes 1622024 | tf_op jit(solution)/shard_map/ppermute | solution.py:32
  53.5 9.4 %collective-permute-start.15 = (bf16[64,4224]{1,0:T(8,128)(2,1)S(1)}, bf16[64,4224]{1,0:T(8,128)(2,1)S(1)}, u32[]{:S(2)}, u32[]{:S(2)}) collective-permute-start(bf16[64,4224]{1,0:T(8,128)(2,1)S(1)} %constant_dynamic-update-slice_fusion.5.refs_1_), channel_id=1, source_target_pairs={{0,96},{1,7},{2,98},{3,1},{4,100},{5,3},{6,102},{7,5},{8,104},{9,1... | collective-permute-start | bytes 1622024 | tf_op jit(solution)/shard_map/ppermute | solution.py:32
  53.5 10.6 %collective-permute-start.16 = (bf16[64,4224]{1,0:T(8,128)(2,1)S(1)}, bf16[64,4224]{1,0:T(8,128)(2,1)S(1)}, u32[]{:S(2)}, u32[]{:S(2)}) collective-permute-start(bf16[64,4224]{1,0:T(8,128)(2,1)S(1)} %constant_dynamic-update-slice_fusion.refs_0_), channel_id=1, source_target_pairs={{0,32},{1,3},{2,34},{3,5},{4,36},{5,7},{6,38},{7,1},{8,40},{9,11},... | collective-permute-start | bytes 1622024 | tf_op jit(solution)/shard_map/ppermute | solution.py:32
  55.5 16.6 %collective-permute-start.13 = (bf16[128,4096]{1,0:T(8,128)(2,1)S(1)}, bf16[128,4096]{1,0:T(8,128)(2,1)S(1)}, u32[]{:S(2)}, u32[]{:S(2)}) collective-permute-start(bf16[128,4096]{1,0:T(8,128)(2,1)S(1)} %get-tuple-element.28), channel_id=1, source_target_pairs={{0,1},{1,0},{2,3},{3,2},{4,5},{5,4},{6,7},{7,6},{8,9},{9,8},{10,11... | collective-permute-start | bytes 3145736 | tf_op jit(solution)/shard_map/ppermute | solution.py:36
  64.5 27.4 %collective-permute-start.8 = (bf16[128,4096]{1,0:T(8,128)(2,1)S(1)}, bf16[128,4096]{1,0:T(8,128)(2,1)S(1)}, u32[]{:S(2)}, u32[]{:S(2)}) collective-permute-start(bf16[128,4096]{1,0:T(8,128)(2,1)S(1)} %get-tuple-element.24), channel_id=1, source_target_pairs={{0,1},{1,0},{2,3},{3,2},{4,5},{5,4},{6,7},{7,6},{8,9},{9,8},{10,11... | collective-permute-start | bytes 3145736 | tf_op jit(solution)/shard_map/ppermute | solution.py:36
  64.6 11.1 %collective-permute-start.24 = (bf16[128,4096]{1,0:T(8,128)(2,1)S(1)}, bf16[128,4096]{1,0:T(8,128)(2,1)S(1)}, u32[]{:S(2)}, u32[]{:S(2)}) collective-permute-start(bf16[128,4096]{1,0:T(8,128)(2,1)S(1)} %get-tuple-element.31), channel_id=1, source_target_pairs={{0,1},{1,0},{2,3},{3,2},{4,5},{5,4},{6,7},{7,6},{8,9},{9,8},{10,11... | collective-permute-start | bytes 3145736 | tf_op jit(solution)/shard_map/ppermute | solution.py:36
  71.8 4.1 %collective-permute-start.23 = (bf16[128,4096]{1,0:T(8,128)(2,1)S(1)}, bf16[128,4096]{1,0:T(8,128)(2,1)S(1)}, u32[]{:S(2)}, u32[]{:S(2)}) collective-permute-start(bf16[128,4096]{1,0:T(8,128)(2,1)S(1)} %get-tuple-element.35), channel_id=1, source_target_pairs={{0,1},{1,0},{2,3},{3,2},{4,5},{5,4},{6,7},{7,6},{8,9},{9,8},{10,11... | collective-permute-start | bytes 3145736 | tf_op jit(solution)/shard_map/ppermute | solution.py:36
  72.3 19.9 %collective-permute-start.14 = (bf16[64,4096]{1,0:T(8,128)(2,1)S(1)}, bf16[64,4096]{1,0:T(8,128)(2,1)S(1)}, u32[]{:S(2)}, u32[]{:S(2)}) collective-permute-start(bf16[64,4096]{1,0:T(8,128)(2,1)S(1)} %get-tuple-element.37), channel_id=1, source_target_pairs={{0,32},{1,3},{2,34},{3,5},{4,36},{5,7},{6,38},{7,1},{8,40},{9,11},... | collective-permute-start | bytes 1572872 | tf_op jit(solution)/shard_map/ppermute | solution.py:32
  73.2 19.0 %collective-permute-start.28 = (bf16[64,4096]{1,0:T(8,128)(2,1)S(1)}, bf16[64,4096]{1,0:T(8,128)(2,1)S(1)}, u32[]{:S(2)}, u32[]{:S(2)}) collective-permute-start(bf16[64,4096]{1,0:T(8,128)(2,1)S(1)} %get-tuple-element.38), channel_id=1, source_target_pairs={{0,96},{1,7},{2,98},{3,1},{4,100},{5,3},{6,102},{7,5},{8,104},{9,1... | collective-permute-start | bytes 1572872 | tf_op jit(solution)/shard_map/ppermute | solution.py:32
  75.9 12.1 %collective-permute-start.25 = (bf16[64,4096]{1,0:T(8,128)(2,1)S(1)}, bf16[64,4096]{1,0:T(8,128)(2,1)S(1)}, u32[]{:S(2)}, u32[]{:S(2)}) collective-permute-start(bf16[64,4096]{1,0:T(8,128)(2,1)S(1)} %get-tuple-element.39), channel_id=1, source_target_pairs={{0,96},{1,7},{2,98},{3,1},{4,100},{5,3},{6,102},{7,5},{8,104},{9,1... | collective-permute-start | bytes 1572872 | tf_op jit(solution)/shard_map/ppermute | solution.py:32
  76.0 12.4 %collective-permute-start.29 = (bf16[64,4096]{1,0:T(8,128)(2,1)S(1)}, bf16[64,4096]{1,0:T(8,128)(2,1)S(1)}, u32[]{:S(2)}, u32[]{:S(2)}) collective-permute-start(bf16[64,4096]{1,0:T(8,128)(2,1)S(1)} %get-tuple-element.40), channel_id=1, source_target_pairs={{0,32},{1,3},{2,34},{3,5},{4,36},{5,7},{6,38},{7,1},{8,40},{9,11},... | collective-permute-start | bytes 1572872 | tf_op jit(solution)/shard_map/ppermute | solution.py:32
  88.6 10.0 %collective-permute-start.26 = (bf16[64,4096]{1,0:T(8,128)(2,1)S(1)}, bf16[64,4096]{1,0:T(8,128)(2,1)S(1)}, u32[]{:S(2)}, u32[]{:S(2)}) collective-permute-start(bf16[64,4096]{1,0:T(8,128)(2,1)S(1)} %get-tuple-element.44), channel_id=1, source_target_pairs={{0,96},{1,7},{2,98},{3,1},{4,100},{5,3},{6,102},{7,5},{8,104},{9,1... | collective-permute-start | bytes 1572872 | tf_op jit(solution)/shard_map/ppermute | solution.py:32
  91.9 10.4 %collective-permute-start.30 = (bf16[64,4096]{1,0:T(8,128)(2,1)S(1)}, bf16[64,4096]{1,0:T(8,128)(2,1)S(1)}, u32[]{:S(2)}, u32[]{:S(2)}) collective-permute-start(bf16[64,4096]{1,0:T(8,128)(2,1)S(1)} %get-tuple-element.45), channel_id=1, source_target_pairs={{0,32},{1,3},{2,34},{3,5},{4,36},{5,7},{6,38},{7,1},{8,40},{9,11},... | collective-permute-start | bytes 1572872 | tf_op jit(solution)/shard_map/ppermute | solution.py:32
  102.6 7.7 %collective-permute-start.27 = (bf16[32,4096]{1,0:T(8,128)(2,1)S(1)}, bf16[32,4096]{1,0:T(8,128)(2,1)S(1)}, u32[]{:S(2)}, u32[]{:S(2)}) collective-permute-start(bf16[32,4096]{1,0:T(8,128)(2,1)S(1)} %get-tuple-element.43), channel_id=1, source_target_pairs={{0,8},{1,33},{2,10},{3,35},{4,12},{5,37},{6,14},{7,39},{8,16},{9,4... | collective-permute-start | bytes 786440 | tf_op jit(solution)/shard_map/ppermute | solution.py:32
  104.3 9.9 %collective-permute-start.31 = (bf16[32,4096]{1,0:T(8,128)(2,1)S(1)}, bf16[32,4096]{1,0:T(8,128)(2,1)S(1)}, u32[]{:S(2)}, u32[]{:S(2)}) collective-permute-start(bf16[32,4096]{1,0:T(8,128)(2,1)S(1)} %get-tuple-element.41), channel_id=1, source_target_pairs={{0,16},{1,65},{2,18},{3,67},{4,20},{5,69},{6,22},{7,71},{8,24},{9,... | collective-permute-start | bytes 786440 | tf_op jit(solution)/shard_map/ppermute | solution.py:32
  107.1 7.2 %collective-permute-start.32 = (bf16[32,4096]{1,0:T(8,128)(2,1)S(1)}, bf16[32,4096]{1,0:T(8,128)(2,1)S(1)}, u32[]{:S(2)}, u32[]{:S(2)}) collective-permute-start(bf16[32,4096]{1,0:T(8,128)(2,1)S(1)} %get-tuple-element.42), channel_id=1, source_target_pairs={{0,24},{1,97},{2,26},{3,99},{4,28},{5,101},{6,30},{7,103},{8,0},{9... | collective-permute-start | bytes 786440 | tf_op jit(solution)/shard_map/ppermute | solution.py:32
  114.5 6.2 %collective-permute-start.33 = (bf16[8,4096]{1,0:T(8,128)(2,1)S(1)}, bf16[8,4096]{1,0:T(8,128)(2,1)S(1)}, u32[]{:S(2)}, u32[]{:S(2)}) collective-permute-start(bf16[8,4096]{1,0:T(8,128)(2,1)S(1)} %get-tuple-element.46), channel_id=1, source_target_pairs={{0,2},{1,9},{2,4},{3,11},{4,6},{5,13},{6,0},{7,15},{8,10},{9,17},{... | collective-permute-start | bytes 196616 | tf_op jit(solution)/shard_map/ppermute | solution.py:32
  114.5 6.2 %collective-permute-start.34 = (bf16[8,4096]{1,0:T(8,128)(2,1)S(1)}, bf16[8,4096]{1,0:T(8,128)(2,1)S(1)}, u32[]{:S(2)}, u32[]{:S(2)}) collective-permute-start(bf16[8,4096]{1,0:T(8,128)(2,1)S(1)} %get-tuple-element.48), channel_id=1, source_target_pairs={{0,4},{1,17},{2,6},{3,19},{4,0},{5,21},{6,2},{7,23},{8,12},{9,25},... | collective-permute-start | bytes 196616 | tf_op jit(solution)/shard_map/ppermute | solution.py:32
  116.3 5.3 %collective-permute-start.35 = (bf16[8,4096]{1,0:T(8,128)(2,1)S(1)}, bf16[8,4096]{1,0:T(8,128)(2,1)S(1)}, u32[]{:S(2)}, u32[]{:S(2)}) collective-permute-start(bf16[8,4096]{1,0:T(8,128)(2,1)S(1)} %get-tuple-element.47), channel_id=1, source_target_pairs={{0,6},{1,25},{2,0},{3,27},{4,2},{5,29},{6,4},{7,31},{8,14},{9,1},{... | collective-permute-start | bytes 196616 | tf_op jit(solution)/shard_map/ppermute | solution.py:32
  (4 other events, 9.9 us)

commit v3 on v2

--- a/solution.py
+++ b/solution.py
@@ -8,7 +8,7 @@
 from jax.sharding import PartitionSpec as P
 
 
-DIMS = ((2, 1, 0), (1, 0, 2))
+DIMS = ((1, 2, 0), (0, 1, 2))
 AXES = ("attn", "expert")
 NODES = [(z, y, x, core) for z in range(4) for y in range(4) for x in range(4) for core in range(2)]
 
@@ -43,32 +43,33 @@
     return total.astype(jnp.bfloat16)
 
 
-def load_kernel(count, *refs):
-    sources, targets, sems = refs[:count], refs[count : 2 * count], refs[2 * count]
-    copies = [pltpu.make_async_copy(sources[i], targets[i], sems.at[i]) for i in range(count)]
+def load_kernel(expert, whole_ref, down_ref, held_ref, kept_ref, sems):
+    copies = [
+        pltpu.make_async_copy(whole_ref, held_ref, sems.at[0]),
+        pltpu.make_async_copy(down_ref.at[expert], kept_ref, sems.at[1]),
+    ]
     for copy in copies:
         copy.start()
     for copy in copies:
         copy.wait()
 
 
-def loaded(*weights):
-    count = len(weights)
+def loaded(whole, w_down, expert):
     return pl.pallas_call(
-        functools.partial(load_kernel, count),
-        out_shape=[pltpu.VMEM(v.shape, v.dtype) for v in weights],
-        in_specs=[pl.BlockSpec(memory_space=pltpu.HBM)] * count,
-        out_specs=[pl.BlockSpec(memory_space=pltpu.VMEM)] * count,
-        scratch_shapes=[pltpu.SemaphoreType.DMA((count,))],
+        functools.partial(load_kernel, expert),
+        out_shape=[pltpu.VMEM(whole.shape, whole.dtype), pltpu.VMEM(w_down.shape[1:], w_down.dtype)],
+        in_specs=[pl.BlockSpec(memory_space=pltpu.HBM)] * 2,
+        out_specs=[pl.BlockSpec(memory_space=pltpu.VMEM)] * 2,
+        scratch_shapes=[pltpu.SemaphoreType.DMA((2,))],
         compiler_params=pltpu.CompilerParams(vmem_limit_bytes=1 << 20),
-        cost_estimate=pl.CostEstimate(flops=0, bytes_accessed=16_000_000, transcendentals=0),
-    )(*[pltpu.with_memory_space_constraint(v, pltpu.HBM) for v in weights])
+        cost_estimate=pl.CostEstimate(flops=0, bytes_accessed=20_000_000, transcendentals=0),
+    )(*[pltpu.with_memory_space_constraint(v, pltpu.HBM) for v in (whole, w_down)])
 
 
 def expert_kernel(counts, local, width, hidden, *refs):
     pieces = refs[: len(counts)]
-    gate_ref, up_ref, down_ref = refs[len(counts) : len(counts) + 3]
-    own_ref, other_ref, rows_ref, hidden_ref = refs[len(counts) + 3 :]
+    gate_ref, up_ref, *down_refs = refs[len(counts) : len(counts) + 2 + local]
+    own_ref, other_ref, rows_ref, hidden_ref = refs[len(counts) + 2 + local :]
     start = 0
     for count, piece in zip(counts, pieces):
         rows_ref[start : start + count, :] = piece[...]
@@ -97,18 +98,19 @@
             hidden_ref[:, at : at + 128] = value.astype(jnp.bfloat16)
     half = own_ref.shape[0]
 
-    result = jnp.dot(hidden_ref[...], down_ref[...], preferred_element_type=jnp.float32)
+    down = jnp.concatenate([ref[...] for ref in down_refs], axis=0)
+    result = jnp.dot(hidden_ref[...], down, preferred_element_type=jnp.float32)
     result = result.astype(jnp.bfloat16)
     own_ref[...] = result[:half]
     other_ref[...] = result[half:]
 
 
-def experts(pieces, w_gate, w_up, w_down):
+def experts(pieces, w_gate, w_up, *w_down):
     counts = tuple(piece.shape[0] for piece in pieces)
     total = sum(counts)
     local, width, hidden = w_gate.shape
     vmem = pl.BlockSpec(memory_space=pltpu.VMEM)
-    held = [pltpu.with_memory_space_constraint(v, pltpu.VMEM) for v in (*pieces, w_gate, w_up, w_down)]
+    held = [pltpu.with_memory_space_constraint(v, pltpu.VMEM) for v in (*pieces, w_gate, w_up, *w_down)]
     return pl.pallas_call(
         functools.partial(expert_kernel, counts, local, width, hidden),
         out_shape=[pltpu.VMEM((total // 2, width), jnp.bfloat16)] * 2,
@@ -132,16 +134,15 @@
 
 
 def per_device(tokens, expert_ids, route_gates, w_gate, w_up, w_down):
-    rows, width = tokens.shape
+    rows, _ = tokens.shape
     picks = expert_ids.shape[1]
-    local, _, hidden = w_gate.shape
     half = 8 * rows
     spare = jnp.zeros((rows, 128 - 2 * picks), tokens.dtype)
     block = jnp.concatenate([tokens, expert_ids.astype(tokens.dtype), route_gates, spare], axis=1)
-    (gate,) = loaded(w_gate)
+    gate, down0 = loaded(w_gate, w_down, 0)
     one = [move(block, -step, 0) for step in (1, 2, 3)]
-    up, down = loaded(w_up, w_down.reshape(local * hidden, width))
-    weights = (gate, up, down)
+    up, down1 = loaded(w_up, w_down, 1)
+    weights = (gate, up, down0, down1)
     block = jnp.concatenate([block] + one, axis=0)
     two = [move(block, -step, 1) for step in (1, 2, 3)]
     near_a = jnp.concatenate([block, two[0]], axis=0)

time: 123 us -> 123 us (level)
  transfers between devices with their start and end apart: 36 -> 36, of which waited for: 21 -> 20; matrix products, arithmetic and copies ran while one was open for 1% -> 1% of each run, Pallas kernels for 23% -> 23%
where the time goes in v3:
time: 123 us
  waiting for transfers between devices  51.3 us (42%)
  starting transfers between devices  39.3 us (32%)
  Pallas kernels  27.7 us (23%)
  other arithmetic  3.12 us (3%)
    ppermute x24, waiting for transfers between devices, move(): return lax.ppermute(value, AXES, pairs(phase, step))  49.4 us
    ppermute x24, starting transfers between devices, move(): return lax.ppermute(value, AXES, pairs(phase, step))  36.1 us
    pallas_call x4, Pallas kernels, experts(): pl.pallas_call(functools.partial(expert_kernel, counts, local, width, hid...  20.3 us
    pallas_call x2, Pallas kernels, loaded(): pl.pallas_call(functools.partial(load_kernel, expert), out_shape=[pltpu.V...  7.46 us
    ppermute x12, starting transfers between devices, swap(): return lax.ppermute(value, AXES, [(i, i ^ 1) for i in range(128)])  3.22 us
  transfers between devices with their start and end apart: 36, of which 20 were waited for; matrix products, arithmetic and copies ran while one was open for 1% of the time, Pallas kernels for 23%

profile of v3, /device:TPU:0, one launch (start us, length us, event | category | flops | bytes accessed | tf_op | source)
XLA Modules:
  0.0 122.8 jit_solution(17174795059369899789)
XLA Ops:
  1.6 3.1 %collective-permute-start = (bf16[8,4224]{1,0:T(8,128)(2,1)S(1)}, bf16[8,4224]{1,0:T(8,128)(2,1)S(1)}, u32[]{:S(2)}, u32[]{:S(2)}) collective-permute-start(bf16[8,4224]{1,0:T(8,128)(2,1)S(1)} %concatenate.13), channel_id=1, source_target_pairs={{0,24},{1,97},{2,26},{3,99},{4,28},{5,101},{6,30},{7,103},{8,0},{9... | collective-permute-start | bytes 202760 | tf_op jit(solution)/shard_map/ppermute | solution.py:32
  5.4 1.0 collective-permute-start.2
  6.7 3.9 %collective-permute-done.1 = bf16[8,4224]{1,0:T(8,128)(2,1)S(1)} collective-permute-done((bf16[8,4224]{1,0:T(8,128)(2,1)S(1)}, bf16[8,4224]{1,0:T(8,128)(2,1)S(1)}, u32[]{:S(2)}, u32[]{:S(2)}) %collective-permute-start.1) | collective-permute-done | bytes 67616 | tf_op jit(solution)/shard_map/ppermute | solution.py:32
  11.3 3.1 %collective-permute-start.4 = (bf16[32,4224]{1,0:T(8,128)(2,1)S(1)}, bf16[32,4224]{1,0:T(8,128)(2,1)S(1)}, u32[]{:S(2)}, u32[]{:S(2)}) collective-permute-start(bf16[32,4224]{1,0:T(8,128)(2,1)S(1)} %pad_maximum_fusion), channel_id=1, source_target_pairs={{0,4},{1,17},{2,6},{3,19},{4,0},{5,21},{6,2},{7,23},{8,12},{9,25},... | collective-permute-start | bytes 811016 | tf_op jit(solution)/shard_map/ppermute | solution.py:32
  15.0 2.6 %collective-permute-start.3 = (bf16[32,4224]{1,0:T(8,128)(2,1)S(1)}, bf16[32,4224]{1,0:T(8,128)(2,1)S(1)}, u32[]{:S(2)}, u32[]{:S(2)}) collective-permute-start(bf16[32,4224]{1,0:T(8,128)(2,1)S(1)} %pad_maximum_fusion), channel_id=1, source_target_pairs={{0,6},{1,25},{2,0},{3,27},{4,2},{5,29},{6,4},{7,31},{8,14},{9,1},{... | collective-permute-start | bytes 811016 | tf_op jit(solution)/shard_map/ppermute | solution.py:32
  17.7 1.7 %collective-permute-done.4 = bf16[32,4224]{1,0:T(8,128)(2,1)S(1)} collective-permute-done((bf16[32,4224]{1,0:T(8,128)(2,1)S(1)}, bf16[32,4224]{1,0:T(8,128)(2,1)S(1)}, u32[]{:S(2)}, u32[]{:S(2)}) %collective-permute-start.4) | collective-permute-done | bytes 270368 | tf_op jit(solution)/shard_map/ppermute | solution.py:32
  19.4 2.9 %collective-permute-done.5 = bf16[32,4224]{1,0:T(8,128)(2,1)S(1)} collective-permute-done((bf16[32,4224]{1,0:T(8,128)(2,1)S(1)}, bf16[32,4224]{1,0:T(8,128)(2,1)S(1)}, u32[]{:S(2)}, u32[]{:S(2)}) %collective-permute-start.5) | collective-permute-done | bytes 270368 | tf_op jit(solution)/shard_map/ppermute | solution.py:32
  23.0 1.9 %collective-permute-start.10 = (bf16[64,4224]{1,0:T(8,128)(2,1)S(1)}, bf16[64,4224]{1,0:T(8,128)(2,1)S(1)}, u32[]{:S(2)}, u32[]{:S(2)}) collective-permute-start(bf16[64,4224]{1,0:T(8,128)(2,1)S(1)} %constant_dynamic-update-slice_fusion.5.refs_1_), channel_id=1, source_target_pairs={{0,32},{1,3},{2,34},{3,5},{4,36},{5,7},{6,38},{7,1},{8,40},{9,11},... | collective-permute-start | bytes 1622024 | tf_op jit(solution)/shard_map/ppermute | solution.py:32
  24.9 2.1 %collective-permute-start.9 = (bf16[64,4224]{1,0:T(8,128)(2,1)S(1)}, bf16[64,4224]{1,0:T(8,128)(2,1)S(1)}, u32[]{:S(2)}, u32[]{:S(2)}) collective-permute-start(bf16[64,4224]{1,0:T(8,128)(2,1)S(1)} %constant_dynamic-update-slice_fusion.refs_0_), channel_id=1, source_target_pairs={{0,96},{1,7},{2,98},{3,1},{4,100},{5,3},{6,102},{7,5},{8,104},{9,1... | collective-permute-start | bytes 1622024 | tf_op jit(solution)/shard_map/ppermute | solution.py:32
  27.0 3.7 %shard_map.64 = (bf16[2,4096,384]{2,1,0:T(8,128)(2,1)S(1)}, bf16[384,4096]{1,0:T(8,128)(2,1)S(1)}) custom-call(bf16[2,4096,384]{2,1,0:T(8,128)(2,1)} %whole_ref.2, bf16[2,384,4096]{2,1,0:T(8,128)(2,1)} %down_ref.3), custom_call_target="tpu_custom_call" | custom-call | bytes 20000000 | tf_op jit(solution)/shard_map/pallas_call | solution.py:58
  30.7 3.7 %shard_map.65 = (bf16[2,4096,384]{2,1,0:T(8,128)(2,1)S(1)}, bf16[384,4096]{1,0:T(8,128)(2,1)S(1)}) custom-call(bf16[2,4096,384]{2,1,0:T(8,128)(2,1)} %whole_ref.3, bf16[2,384,4096]{2,1,0:T(8,128)(2,1)} %down_ref.3), custom_call_target="tpu_custom_call" | custom-call | bytes 20000000 | tf_op jit(solution)/shard_map/pallas_call | solution.py:58
  34.5 5.1 %shard_map.66 = (bf16[128,4096]{1,0:T(8,128)(2,1)S(1)}, bf16[128,4096]{1,0:T(8,128)(2,1)S(1)}) custom-call(bf16[64,4224]{1,0:T(8,128)(2,1)S(1)} %constant_dynamic-update-slice_fusion.refs_0_, bf16[64,4224]{1,0:T(8,128)(2,1)S(1)} %constant_dynamic-update-slice_fusion.5.refs_1_, bf16[64,4224]{1,0:T(8,128)(2,1)S(1)} %collective-permute-done.6.refs_2_, ...), custom_call_target="tpu_custom_call" | custom-call | flops 4831838208 | bytes 4194304 | tf_op jit(solution)/shard_map/pallas_call | solution.py:114
  40.2 2.3 %collective-permute-start.17 = (bf16[64,4224]{1,0:T(8,128)(2,1)S(1)}, bf16[64,4224]{1,0:T(8,128)(2,1)S(1)}, u32[]{:S(2)}, u32[]{:S(2)}) collective-permute-start(bf16[64,4224]{1,0:T(8,128)(2,1)S(1)} %collective-permute-done.9.refs_0_), channel_id=1, source_target_pairs={{0,96},{1,7},{2,98},{3,1},{4,100},{5,3},{6,102},{7,5},{8,104},{9,1... | collective-permute-start | bytes 1622024 | tf_op jit(solution)/shard_map/ppermute | solution.py:32
  42.5 5.1 %shard_map.67 = (bf16[128,4096]{1,0:T(8,128)(2,1)S(1)}, bf16[128,4096]{1,0:T(8,128)(2,1)S(1)}) custom-call(bf16[64,4224]{1,0:T(8,128)(2,1)S(1)} %collective-permute-done.9.refs_0_, bf16[64,4224]{1,0:T(8,128)(2,1)S(1)} %collective-permute-done.10.refs_1_, bf16[64,4224]{1,0:T(8,128)(2,1)S(1)} %collective-permute-done.11.refs_2_, ...), custom_call_target="tpu_custom_call" | custom-call | flops 4831838208 | bytes 4194304 | tf_op jit(solution)/shard_map/pallas_call | solution.py:114
  47.6 1.9 %collective-permute-done.17.refs_0_ = bf16[64,4224]{1,0:T(8,128)(2,1)S(1)} collective-permute-done((bf16[64,4224]{1,0:T(8,128)(2,1)S(1)}, bf16[64,4224]{1,0:T(8,128)(2,1)S(1)}, u32[]{:S(2)}, u32[]{:S(2)}) %collective-permute-start.17) | collective-permute-done | bytes 540704 | tf_op jit(solution)/shard_map/ppermute | solution.py:32
  49.5 3.5 %collective-permute-done.18.refs_1_ = bf16[64,4224]{1,0:T(8,128)(2,1)S(1)} collective-permute-done((bf16[64,4224]{1,0:T(8,128)(2,1)S(1)}, bf16[64,4224]{1,0:T(8,128)(2,1)S(1)}, u32[]{:S(2)}, u32[]{:S(2)}) %collective-permute-start.18) | collective-permute-done | bytes 540704 | tf_op jit(solution)/shard_map/ppermute | solution.py:32
  54.0 1.7 %collective-permute-start.16 = (bf16[64,4224]{1,0:T(8,128)(2,1)S(1)}, bf16[64,4224]{1,0:T(8,128)(2,1)S(1)}, u32[]{:S(2)}, u32[]{:S(2)}) collective-permute-start(bf16[64,4224]{1,0:T(8,128)(2,1)S(1)} %constant_dynamic-update-slice_fusion.refs_0_), channel_id=1, source_target_pairs={{0,32},{1,3},{2,34},{3,5},{4,36},{5,7},{6,38},{7,1},{8,40},{9,11},... | collective-permute-start | bytes 1622024 | tf_op jit(solution)/shard_map/ppermute | solution.py:32
  55.8 5.1 %shard_map.68 = (bf16[128,4096]{1,0:T(8,128)(2,1)S(1)}, bf16[128,4096]{1,0:T(8,128)(2,1)S(1)}) custom-call(bf16[64,4224]{1,0:T(8,128)(2,1)S(1)} %collective-permute-done.17.refs_0_, bf16[64,4224]{1,0:T(8,128)(2,1)S(1)} %collective-permute-done.18.refs_1_, bf16[64,4224]{1,0:T(8,128)(2,1)S(1)} %collective-permute-done.19.refs_2_, ...), custom_call_target="tpu_custom_call" | custom-call | flops 4831838208 | bytes 4194304 | tf_op jit(solution)/shard_map/pallas_call | solution.py:114
  60.9 2.1 %collective-permute-done.15.refs_0_ = bf16[64,4224]{1,0:T(8,128)(2,1)S(1)} collective-permute-done((bf16[64,4224]{1,0:T(8,128)(2,1)S(1)}, bf16[64,4224]{1,0:T(8,128)(2,1)S(1)}, u32[]{:S(2)}, u32[]{:S(2)}) %collective-permute-start.15) | collective-permute-done | bytes 540704 | tf_op jit(solution)/shard_map/ppermute | solution.py:32
  63.0 1.6 %collective-permute-done.16.refs_1_ = bf16[64,4224]{1,0:T(8,128)(2,1)S(1)} collective-permute-done((bf16[64,4224]{1,0:T(8,128)(2,1)S(1)}, bf16[64,4224]{1,0:T(8,128)(2,1)S(1)}, u32[]{:S(2)}, u32[]{:S(2)}) %collective-permute-start.16) | collective-permute-done | bytes 540704 | tf_op jit(solution)/shard_map/ppermute | solution.py:32
  67.3 5.1 %shard_map.69 = (bf16[128,4096]{1,0:T(8,128)(2,1)S(1)}, bf16[128,4096]{1,0:T(8,128)(2,1)S(1)}) custom-call(bf16[64,4224]{1,0:T(8,128)(2,1)S(1)} %collective-permute-done.15.refs_0_, bf16[64,4224]{1,0:T(8,128)(2,1)S(1)} %collective-permute-done.16.refs_1_, bf16[64,4224]{1,0:T(8,128)(2,1)S(1)} %collective-permute-done.21.refs_2_, ...), custom_call_target="tpu_custom_call" | custom-call | flops 4831838208 | bytes 4194304 | tf_op jit(solution)/shard_map/pallas_call | solution.py:114
  73.3 3.1 %collective-permute-start.28 = (bf16[64,4096]{1,0:T(8,128)(2,1)S(1)}, bf16[64,4096]{1,0:T(8,128)(2,1)S(1)}, u32[]{:S(2)}, u32[]{:S(2)}) collective-permute-start(bf16[64,4096]{1,0:T(8,128)(2,1)S(1)} %get-tuple-element.42), channel_id=1, source_target_pairs={{0,96},{1,7},{2,98},{3,1},{4,100},{5,3},{6,102},{7,5},{8,104},{9,1... | collective-permute-start | bytes 1572872 | tf_op jit(solution)/shard_map/ppermute | solution.py:32
  76.7 2.0 %collective-permute-start.29 = (bf16[64,4096]{1,0:T(8,128)(2,1)S(1)}, bf16[64,4096]{1,0:T(8,128)(2,1)S(1)}, u32[]{:S(2)}, u32[]{:S(2)}) collective-permute-start(bf16[64,4096]{1,0:T(8,128)(2,1)S(1)} %get-tuple-element.44), channel_id=1, source_target_pairs={{0,32},{1,3},{2,34},{3,5},{4,36},{5,7},{6,38},{7,1},{8,40},{9,11},... | collective-permute-start | bytes 1572872 | tf_op jit(solution)/shard_map/ppermute | solution.py:32
  79.0 9.7 %collective-permute-done.25 = bf16[64,4096]{1,0:T(8,128)(2,1)S(1)} collective-permute-done((bf16[64,4096]{1,0:T(8,128)(2,1)S(1)}, bf16[64,4096]{1,0:T(8,128)(2,1)S(1)}, u32[]{:S(2)}, u32[]{:S(2)}) %collective-permute-start.25) | collective-permute-done | bytes 524320 | tf_op jit(solution)/shard_map/ppermute | solution.py:32
  89.4 3.3 %collective-permute-start.26 = (bf16[64,4096]{1,0:T(8,128)(2,1)S(1)}, bf16[64,4096]{1,0:T(8,128)(2,1)S(1)}, u32[]{:S(2)}, u32[]{:S(2)}) collective-permute-start(bf16[64,4096]{1,0:T(8,128)(2,1)S(1)} %get-tuple-element.48), channel_id=1, source_target_pairs={{0,96},{1,7},{2,98},{3,1},{4,100},{5,3},{6,102},{7,5},{8,104},{9,1... | collective-permute-start | bytes 1572872 | tf_op jit(solution)/shard_map/ppermute | solution.py:32
  93.0 6.4 %collective-permute-done.26 = bf16[64,4096]{1,0:T(8,128)(2,1)S(1)} collective-permute-done((bf16[64,4096]{1,0:T(8,128)(2,1)S(1)}, bf16[64,4096]{1,0:T(8,128)(2,1)S(1)}, u32[]{:S(2)}, u32[]{:S(2)}) %collective-permute-start.26) | collective-permute-done | bytes 524320 | tf_op jit(solution)/shard_map/ppermute | solution.py:32
  99.4 3.7 %collective-permute-done.30 = bf16[64,4096]{1,0:T(8,128)(2,1)S(1)} collective-permute-done((bf16[64,4096]{1,0:T(8,128)(2,1)S(1)}, bf16[64,4096]{1,0:T(8,128)(2,1)S(1)}, u32[]{:S(2)}, u32[]{:S(2)}) %collective-permute-start.30) | collective-permute-done | bytes 524320 | tf_op jit(solution)/shard_map/ppermute | solution.py:32
  104.1 2.4 %collective-permute-start.31 = (bf16[32,4096]{1,0:T(8,128)(2,1)S(1)}, bf16[32,4096]{1,0:T(8,128)(2,1)S(1)}, u32[]{:S(2)}, u32[]{:S(2)}) collective-permute-start(bf16[32,4096]{1,0:T(8,128)(2,1)S(1)} %get-tuple-element.45), channel_id=1, source_target_pairs={{0,4},{1,17},{2,6},{3,19},{4,0},{5,21},{6,2},{7,23},{8,12},{9,25},... | collective-permute-start | bytes 786440 | tf_op jit(solution)/shard_map/ppermute | solution.py:32
  107.3 6.6 %collective-permute-done.27 = bf16[32,4096]{1,0:T(8,128)(2,1)S(1)} collective-permute-done((bf16[32,4096]{1,0:T(8,128)(2,1)S(1)}, bf16[32,4096]{1,0:T(8,128)(2,1)S(1)}, u32[]{:S(2)}, u32[]{:S(2)}) %collective-permute-start.27) | collective-permute-done | bytes 262176 | tf_op jit(solution)/shard_map/ppermute | solution.py:32
  115.1 2.0 %collective-permute-start.34 = (bf16[8,4096]{1,0:T(8,128)(2,1)S(1)}, bf16[8,4096]{1,0:T(8,128)(2,1)S(1)}, u32[]{:S(2)}, u32[]{:S(2)}) collective-permute-start(bf16[8,4096]{1,0:T(8,128)(2,1)S(1)} %get-tuple-element.52), channel_id=1, source_target_pairs={{0,16},{1,65},{2,18},{3,67},{4,20},{5,69},{6,22},{7,71},{8,24},{9,... | collective-permute-start | bytes 196616 | tf_op jit(solution)/shard_map/ppermute | solution.py:32
  117.1 1.9 %collective-permute-start.35 = (bf16[8,4096]{1,0:T(8,128)(2,1)S(1)}, bf16[8,4096]{1,0:T(8,128)(2,1)S(1)}, u32[]{:S(2)}, u32[]{:S(2)}) collective-permute-start(bf16[8,4096]{1,0:T(8,128)(2,1)S(1)} %get-tuple-element.51), channel_id=1, source_target_pairs={{0,24},{1,97},{2,26},{3,99},{4,28},{5,101},{6,30},{7,103},{8,0},{9... | collective-permute-start | bytes 196616 | tf_op jit(solution)/shard_map/ppermute | solution.py:32
  119.0 2.2 %collective-permute-done.33 = bf16[8,4096]{1,0:T(8,128)(2,1)S(1)} collective-permute-done((bf16[8,4096]{1,0:T(8,128)(2,1)S(1)}, bf16[8,4096]{1,0:T(8,128)(2,1)S(1)}, u32[]{:S(2)}, u32[]{:S(2)}) %collective-permute-start.33) | collective-permute-done | bytes 65568 | tf_op jit(solution)/shard_map/ppermute | solution.py:32
  (66 shorter events, 16.0 us)
Async XLA Ops:
  1.6 5.1 %collective-permute-start = (bf16[8,4224]{1,0:T(8,128)(2,1)S(1)}, bf16[8,4224]{1,0:T(8,128)(2,1)S(1)}, u32[]{:S(2)}, u32[]{:S(2)}) collective-permute-start(bf16[8,4224]{1,0:T(8,128)(2,1)S(1)} %concatenate.13), channel_id=1, source_target_pairs={{0,24},{1,97},{2,26},{3,99},{4,28},{5,101},{6,30},{7,103},{8,0},{9... | collective-permute-start | bytes 202760 | tf_op jit(solution)/shard_map/ppermute | solution.py:32
  4.7 5.8 %collective-permute-start.1 = (bf16[8,4224]{1,0:T(8,128)(2,1)S(1)}, bf16[8,4224]{1,0:T(8,128)(2,1)S(1)}, u32[]{:S(2)}, u32[]{:S(2)}) collective-permute-start(bf16[8,4224]{1,0:T(8,128)(2,1)S(1)} %concatenate.13), channel_id=1, source_target_pairs={{0,16},{1,65},{2,18},{3,67},{4,20},{5,69},{6,22},{7,71},{8,24},{9,... | collective-permute-start | bytes 202760 | tf_op jit(solution)/shard_map/ppermute | solution.py:32
  5.4 5.9 %collective-permute-start.2 = (bf16[8,4224]{1,0:T(8,128)(2,1)S(1)}, bf16[8,4224]{1,0:T(8,128)(2,1)S(1)}, u32[]{:S(2)}, u32[]{:S(2)}) collective-permute-start(bf16[8,4224]{1,0:T(8,128)(2,1)S(1)} %concatenate.13), channel_id=1, source_target_pairs={{0,8},{1,33},{2,10},{3,35},{4,12},{5,37},{6,14},{7,39},{8,16},{9,4... | collective-permute-start | bytes 202760 | tf_op jit(solution)/shard_map/ppermute | solution.py:32
  11.3 8.1 %collective-permute-start.4 = (bf16[32,4224]{1,0:T(8,128)(2,1)S(1)}, bf16[32,4224]{1,0:T(8,128)(2,1)S(1)}, u32[]{:S(2)}, u32[]{:S(2)}) collective-permute-start(bf16[32,4224]{1,0:T(8,128)(2,1)S(1)} %pad_maximum_fusion), channel_id=1, source_target_pairs={{0,4},{1,17},{2,6},{3,19},{4,0},{5,21},{6,2},{7,23},{8,12},{9,25},... | collective-permute-start | bytes 811016 | tf_op jit(solution)/shard_map/ppermute | solution.py:32
  14.4 7.8 %collective-permute-start.5 = (bf16[32,4224]{1,0:T(8,128)(2,1)S(1)}, bf16[32,4224]{1,0:T(8,128)(2,1)S(1)}, u32[]{:S(2)}, u32[]{:S(2)}) collective-permute-start(bf16[32,4224]{1,0:T(8,128)(2,1)S(1)} %pad_maximum_fusion), channel_id=1, source_target_pairs={{0,2},{1,9},{2,4},{3,11},{4,6},{5,13},{6,0},{7,15},{8,10},{9,17},{... | collective-permute-start | bytes 811016 | tf_op jit(solution)/shard_map/ppermute | solution.py:32
  15.0 7.4 %collective-permute-start.3 = (bf16[32,4224]{1,0:T(8,128)(2,1)S(1)}, bf16[32,4224]{1,0:T(8,128)(2,1)S(1)}, u32[]{:S(2)}, u32[]{:S(2)}) collective-permute-start(bf16[32,4224]{1,0:T(8,128)(2,1)S(1)} %pad_maximum_fusion), channel_id=1, source_target_pairs={{0,6},{1,25},{2,0},{3,27},{4,2},{5,29},{6,4},{7,31},{8,14},{9,1},{... | collective-permute-start | bytes 811016 | tf_op jit(solution)/shard_map/ppermute | solution.py:32
  22.3 12.2 %collective-permute-start.7 = (bf16[64,4224]{1,0:T(8,128)(2,1)S(1)}, bf16[64,4224]{1,0:T(8,128)(2,1)S(1)}, u32[]{:S(2)}, u32[]{:S(2)}) collective-permute-start(bf16[64,4224]{1,0:T(8,128)(2,1)S(1)} %constant_dynamic-update-slice_fusion.5.refs_1_), channel_id=1, source_target_pairs={{0,1},{1,0},{2,3},{3,2},{4,5},{5,4},{6,7},{7,6},{8,9},{9,8},{10,11... | collective-permute-start | bytes 1622024 | tf_op jit(solution)/shard_map/ppermute | solution.py:36
  22.4 12.1 %collective-permute-start.6 = (bf16[64,4224]{1,0:T(8,128)(2,1)S(1)}, bf16[64,4224]{1,0:T(8,128)(2,1)S(1)}, u32[]{:S(2)}, u32[]{:S(2)}) collective-permute-start(bf16[64,4224]{1,0:T(8,128)(2,1)S(1)} %constant_dynamic-update-slice_fusion.refs_0_), channel_id=1, source_target_pairs={{0,1},{1,0},{2,3},{3,2},{4,5},{5,4},{6,7},{7,6},{8,9},{9,8},{10,11... | collective-permute-start | bytes 1622024 | tf_op jit(solution)/shard_map/ppermute | solution.py:36
  23.0 16.6 %collective-permute-start.10 = (bf16[64,4224]{1,0:T(8,128)(2,1)S(1)}, bf16[64,4224]{1,0:T(8,128)(2,1)S(1)}, u32[]{:S(2)}, u32[]{:S(2)}) collective-permute-start(bf16[64,4224]{1,0:T(8,128)(2,1)S(1)} %constant_dynamic-update-slice_fusion.5.refs_1_), channel_id=1, source_target_pairs={{0,32},{1,3},{2,34},{3,5},{4,36},{5,7},{6,38},{7,1},{8,40},{9,11},... | collective-permute-start | bytes 1622024 | tf_op jit(solution)/shard_map/ppermute | solution.py:32
  24.9 14.7 %collective-permute-start.9 = (bf16[64,4224]{1,0:T(8,128)(2,1)S(1)}, bf16[64,4224]{1,0:T(8,128)(2,1)S(1)}, u32[]{:S(2)}, u32[]{:S(2)}) collective-permute-start(bf16[64,4224]{1,0:T(8,128)(2,1)S(1)} %constant_dynamic-update-slice_fusion.refs_0_), channel_id=1, source_target_pairs={{0,96},{1,7},{2,98},{3,1},{4,100},{5,3},{6,102},{7,5},{8,104},{9,1... | collective-permute-start | bytes 1622024 | tf_op jit(solution)/shard_map/ppermute | solution.py:32
  39.6 2.9 %collective-permute-start.11 = (bf16[64,4224]{1,0:T(8,128)(2,1)S(1)}, bf16[64,4224]{1,0:T(8,128)(2,1)S(1)}, u32[]{:S(2)}, u32[]{:S(2)}) collective-permute-start(bf16[64,4224]{1,0:T(8,128)(2,1)S(1)} %collective-permute-done.9.refs_0_), channel_id=1, source_target_pairs={{0,1},{1,0},{2,3},{3,2},{4,5},{5,4},{6,7},{7,6},{8,9},{9,8},{10,11... | collective-permute-start | bytes 1622024 | tf_op jit(solution)/shard_map/ppermute | solution.py:36
  39.7 2.8 %collective-permute-start.12 = (bf16[64,4224]{1,0:T(8,128)(2,1)S(1)}, bf16[64,4224]{1,0:T(8,128)(2,1)S(1)}, u32[]{:S(2)}, u32[]{:S(2)}) collective-permute-start(bf16[64,4224]{1,0:T(8,128)(2,1)S(1)} %collective-permute-done.10.refs_1_), channel_id=1, source_target_pairs={{0,1},{1,0},{2,3},{3,2},{4,5},{5,4},{6,7},{7,6},{8,9},{9,8},{10,11... | collective-permute-start | bytes 1622024 | tf_op jit(solution)/shard_map/ppermute | solution.py:36
  40.2 9.4 %collective-permute-start.17 = (bf16[64,4224]{1,0:T(8,128)(2,1)S(1)}, bf16[64,4224]{1,0:T(8,128)(2,1)S(1)}, u32[]{:S(2)}, u32[]{:S(2)}) collective-permute-start(bf16[64,4224]{1,0:T(8,128)(2,1)S(1)} %collective-permute-done.9.refs_0_), channel_id=1, source_target_pairs={{0,96},{1,7},{2,98},{3,1},{4,100},{5,3},{6,102},{7,5},{8,104},{9,1... | collective-permute-start | bytes 1622024 | tf_op jit(solution)/shard_map/ppermute | solution.py:32
  42.5 10.6 %collective-permute-start.18 = (bf16[64,4224]{1,0:T(8,128)(2,1)S(1)}, bf16[64,4224]{1,0:T(8,128)(2,1)S(1)}, u32[]{:S(2)}, u32[]{:S(2)}) collective-permute-start(bf16[64,4224]{1,0:T(8,128)(2,1)S(1)} %collective-permute-done.10.refs_1_), channel_id=1, source_target_pairs={{0,32},{1,3},{2,34},{3,5},{4,36},{5,7},{6,38},{7,1},{8,40},{9,11},... | collective-permute-start | bytes 1622024 | tf_op jit(solution)/shard_map/ppermute | solution.py:32
  53.6 9.4 %collective-permute-start.15 = (bf16[64,4224]{1,0:T(8,128)(2,1)S(1)}, bf16[64,4224]{1,0:T(8,128)(2,1)S(1)}, u32[]{:S(2)}, u32[]{:S(2)}) collective-permute-start(bf16[64,4224]{1,0:T(8,128)(2,1)S(1)} %constant_dynamic-update-slice_fusion.5.refs_1_), channel_id=1, source_target_pairs={{0,96},{1,7},{2,98},{3,1},{4,100},{5,3},{6,102},{7,5},{8,104},{9,1... | collective-permute-start | bytes 1622024 | tf_op jit(solution)/shard_map/ppermute | solution.py:32
  54.0 10.6 %collective-permute-start.16 = (bf16[64,4224]{1,0:T(8,128)(2,1)S(1)}, bf16[64,4224]{1,0:T(8,128)(2,1)S(1)}, u32[]{:S(2)}, u32[]{:S(2)}) collective-permute-start(bf16[64,4224]{1,0:T(8,128)(2,1)S(1)} %constant_dynamic-update-slice_fusion.refs_0_), channel_id=1, source_target_pairs={{0,32},{1,3},{2,34},{3,5},{4,36},{5,7},{6,38},{7,1},{8,40},{9,11},... | collective-permute-start | bytes 1622024 | tf_op jit(solution)/shard_map/ppermute | solution.py:32
  55.6 17.2 %collective-permute-start.13 = (bf16[128,4096]{1,0:T(8,128)(2,1)S(1)}, bf16[128,4096]{1,0:T(8,128)(2,1)S(1)}, u32[]{:S(2)}, u32[]{:S(2)}) collective-permute-start(bf16[128,4096]{1,0:T(8,128)(2,1)S(1)} %get-tuple-element.32), channel_id=1, source_target_pairs={{0,1},{1,0},{2,3},{3,2},{4,5},{5,4},{6,7},{7,6},{8,9},{9,8},{10,11... | collective-permute-start | bytes 3145736 | tf_op jit(solution)/shard_map/ppermute | solution.py:36
  65.1 27.7 %collective-permute-start.8 = (bf16[128,4096]{1,0:T(8,128)(2,1)S(1)}, bf16[128,4096]{1,0:T(8,128)(2,1)S(1)}, u32[]{:S(2)}, u32[]{:S(2)}) collective-permute-start(bf16[128,4096]{1,0:T(8,128)(2,1)S(1)} %get-tuple-element.28), channel_id=1, source_target_pairs={{0,1},{1,0},{2,3},{3,2},{4,5},{5,4},{6,7},{7,6},{8,9},{9,8},{10,11... | collective-permute-start | bytes 3145736 | tf_op jit(solution)/shard_map/ppermute | solution.py:36
  65.5 10.9 %collective-permute-start.24 = (bf16[128,4096]{1,0:T(8,128)(2,1)S(1)}, bf16[128,4096]{1,0:T(8,128)(2,1)S(1)}, u32[]{:S(2)}, u32[]{:S(2)}) collective-permute-start(bf16[128,4096]{1,0:T(8,128)(2,1)S(1)} %get-tuple-element.35), channel_id=1, source_target_pairs={{0,1},{1,0},{2,3},{3,2},{4,5},{5,4},{6,7},{7,6},{8,9},{9,8},{10,11... | collective-permute-start | bytes 3145736 | tf_op jit(solution)/shard_map/ppermute | solution.py:36
  72.4 4.4 %collective-permute-start.23 = (bf16[128,4096]{1,0:T(8,128)(2,1)S(1)}, bf16[128,4096]{1,0:T(8,128)(2,1)S(1)}, u32[]{:S(2)}, u32[]{:S(2)}) collective-permute-start(bf16[128,4096]{1,0:T(8,128)(2,1)S(1)} %get-tuple-element.39), channel_id=1, source_target_pairs={{0,1},{1,0},{2,3},{3,2},{4,5},{5,4},{6,7},{7,6},{8,9},{9,8},{10,11... | collective-permute-start | bytes 3145736 | tf_op jit(solution)/shard_map/ppermute | solution.py:36
  73.1 19.9 %collective-permute-start.14 = (bf16[64,4096]{1,0:T(8,128)(2,1)S(1)}, bf16[64,4096]{1,0:T(8,128)(2,1)S(1)}, u32[]{:S(2)}, u32[]{:S(2)}) collective-permute-start(bf16[64,4096]{1,0:T(8,128)(2,1)S(1)} %get-tuple-element.41), channel_id=1, source_target_pairs={{0,32},{1,3},{2,34},{3,5},{4,36},{5,7},{6,38},{7,1},{8,40},{9,11},... | collective-permute-start | bytes 1572872 | tf_op jit(solution)/shard_map/ppermute | solution.py:32
  73.3 19.7 %collective-permute-start.28 = (bf16[64,4096]{1,0:T(8,128)(2,1)S(1)}, bf16[64,4096]{1,0:T(8,128)(2,1)S(1)}, u32[]{:S(2)}, u32[]{:S(2)}) collective-permute-start(bf16[64,4096]{1,0:T(8,128)(2,1)S(1)} %get-tuple-element.42), channel_id=1, source_target_pairs={{0,96},{1,7},{2,98},{3,1},{4,100},{5,3},{6,102},{7,5},{8,104},{9,1... | collective-permute-start | bytes 1572872 | tf_op jit(solution)/shard_map/ppermute | solution.py:32
  76.7 12.1 %collective-permute-start.25 = (bf16[64,4096]{1,0:T(8,128)(2,1)S(1)}, bf16[64,4096]{1,0:T(8,128)(2,1)S(1)}, u32[]{:S(2)}, u32[]{:S(2)}) collective-permute-start(bf16[64,4096]{1,0:T(8,128)(2,1)S(1)} %get-tuple-element.43), channel_id=1, source_target_pairs={{0,96},{1,7},{2,98},{3,1},{4,100},{5,3},{6,102},{7,5},{8,104},{9,1... | collective-permute-start | bytes 1572872 | tf_op jit(solution)/shard_map/ppermute | solution.py:32
  76.7 12.4 %collective-permute-start.29 = (bf16[64,4096]{1,0:T(8,128)(2,1)S(1)}, bf16[64,4096]{1,0:T(8,128)(2,1)S(1)}, u32[]{:S(2)}, u32[]{:S(2)}) collective-permute-start(bf16[64,4096]{1,0:T(8,128)(2,1)S(1)} %get-tuple-element.44), channel_id=1, source_target_pairs={{0,32},{1,3},{2,34},{3,5},{4,36},{5,7},{6,38},{7,1},{8,40},{9,11},... | collective-permute-start | bytes 1572872 | tf_op jit(solution)/shard_map/ppermute | solution.py:32
  89.4 10.0 %collective-permute-start.26 = (bf16[64,4096]{1,0:T(8,128)(2,1)S(1)}, bf16[64,4096]{1,0:T(8,128)(2,1)S(1)}, u32[]{:S(2)}, u32[]{:S(2)}) collective-permute-start(bf16[64,4096]{1,0:T(8,128)(2,1)S(1)} %get-tuple-element.48), channel_id=1, source_target_pairs={{0,96},{1,7},{2,98},{3,1},{4,100},{5,3},{6,102},{7,5},{8,104},{9,1... | collective-permute-start | bytes 1572872 | tf_op jit(solution)/shard_map/ppermute | solution.py:32
  92.7 10.4 %collective-permute-start.30 = (bf16[64,4096]{1,0:T(8,128)(2,1)S(1)}, bf16[64,4096]{1,0:T(8,128)(2,1)S(1)}, u32[]{:S(2)}, u32[]{:S(2)}) collective-permute-start(bf16[64,4096]{1,0:T(8,128)(2,1)S(1)} %get-tuple-element.49), channel_id=1, source_target_pairs={{0,32},{1,3},{2,34},{3,5},{4,36},{5,7},{6,38},{7,1},{8,40},{9,11},... | collective-permute-start | bytes 1572872 | tf_op jit(solution)/shard_map/ppermute | solution.py:32
  103.4 10.5 %collective-permute-start.27 = (bf16[32,4096]{1,0:T(8,128)(2,1)S(1)}, bf16[32,4096]{1,0:T(8,128)(2,1)S(1)}, u32[]{:S(2)}, u32[]{:S(2)}) collective-permute-start(bf16[32,4096]{1,0:T(8,128)(2,1)S(1)} %get-tuple-element.47), channel_id=1, source_target_pairs={{0,2},{1,9},{2,4},{3,11},{4,6},{5,13},{6,0},{7,15},{8,10},{9,17},{... | collective-permute-start | bytes 786440 | tf_op jit(solution)/shard_map/ppermute | solution.py:32
  104.1 9.8 %collective-permute-start.31 = (bf16[32,4096]{1,0:T(8,128)(2,1)S(1)}, bf16[32,4096]{1,0:T(8,128)(2,1)S(1)}, u32[]{:S(2)}, u32[]{:S(2)}) collective-permute-start(bf16[32,4096]{1,0:T(8,128)(2,1)S(1)} %get-tuple-element.45), channel_id=1, source_target_pairs={{0,4},{1,17},{2,6},{3,19},{4,0},{5,21},{6,2},{7,23},{8,12},{9,25},... | collective-permute-start | bytes 786440 | tf_op jit(solution)/shard_map/ppermute | solution.py:32
  106.5 8.3 %collective-permute-start.32 = (bf16[32,4096]{1,0:T(8,128)(2,1)S(1)}, bf16[32,4096]{1,0:T(8,128)(2,1)S(1)}, u32[]{:S(2)}, u32[]{:S(2)}) collective-permute-start(bf16[32,4096]{1,0:T(8,128)(2,1)S(1)} %get-tuple-element.46), channel_id=1, source_target_pairs={{0,6},{1,25},{2,0},{3,27},{4,2},{5,29},{6,4},{7,31},{8,14},{9,1},{... | collective-permute-start | bytes 786440 | tf_op jit(solution)/shard_map/ppermute | solution.py:32
  115.0 6.2 %collective-permute-start.33 = (bf16[8,4096]{1,0:T(8,128)(2,1)S(1)}, bf16[8,4096]{1,0:T(8,128)(2,1)S(1)}, u32[]{:S(2)}, u32[]{:S(2)}) collective-permute-start(bf16[8,4096]{1,0:T(8,128)(2,1)S(1)} %get-tuple-element.50), channel_id=1, source_target_pairs={{0,8},{1,33},{2,10},{3,35},{4,12},{5,37},{6,14},{7,39},{8,16},{9,4... | collective-permute-start | bytes 196616 | tf_op jit(solution)/shard_map/ppermute | solution.py:32
  115.1 6.2 %collective-permute-start.34 = (bf16[8,4096]{1,0:T(8,128)(2,1)S(1)}, bf16[8,4096]{1,0:T(8,128)(2,1)S(1)}, u32[]{:S(2)}, u32[]{:S(2)}) collective-permute-start(bf16[8,4096]{1,0:T(8,128)(2,1)S(1)} %get-tuple-element.52), channel_id=1, source_target_pairs={{0,16},{1,65},{2,18},{3,67},{4,20},{5,69},{6,22},{7,71},{8,24},{9,... | collective-permute-start | bytes 196616 | tf_op jit(solution)/shard_map/ppermute | solution.py:32
  117.1 5.0 %collective-permute-start.35 = (bf16[8,4096]{1,0:T(8,128)(2,1)S(1)}, bf16[8,4096]{1,0:T(8,128)(2,1)S(1)}, u32[]{:S(2)}, u32[]{:S(2)}) collective-permute-start(bf16[8,4096]{1,0:T(8,128)(2,1)S(1)} %get-tuple-element.51), channel_id=1, source_target_pairs={{0,24},{1,97},{2,26},{3,99},{4,28},{5,101},{6,30},{7,103},{8,0},{9... | collective-permute-start | bytes 196616 | tf_op jit(solution)/shard_map/ppermute | solution.py:32
  (4 other events, 9.6 us)
